TPU v7x, 32 devices: a whole 2x2x4 slice. The times are simulated.
32 devices in a mesh: layer: 4 (over x, core), harm: 8 (over z, y).
Axes of the slice: x: 2, y: 2, z: 4, core: 2. Of those that a mesh axis runs over, the one named last changes fastest.
Arguments:
- source: bfloat16 [2, 2048, 128], P(None, 'harm'), may hold values from -6 to 6
- transfer: bfloat16 [4, 2, 2048, 2048], P('layer', None, 'harm'), may hold values from -0.09375 to 0.09375
- fields: bfloat16 [4, 2, 2048, 128], P('layer', None, 'harm'), may hold values from -6 to 6
- orders: int32 [2048], replicated, may hold values from 0 to 2047, each once
Outputs:
- gradients: float32 [4, 2, 4096], P('layer', None, 'harm')
- boundary: bfloat16 [4, 2, 2048, 128], P('layer', None, 'harm')
Inputs may be any that keep to these rules, and one draw needn't show every extreme that they name: `orders`: every value from 0 to 2047 appears exactly once.
All inputs are finite; a program needn't handle non-finite values.
Results may differ from a plain program's by a relative error of at most 0.006.
Values may be sent and summed in bfloat16 or wider, within the bound.
No kernel may reach another device: no remote copies, remote signals or barrier semaphores. Data moves between devices by JAX's collectives and lax.ppermute only.
A program may use at most 64 MiB of HBM per device.

v0:
```python
import math

import jax
import jax.numpy as jnp
from jax import lax
from jax.experimental import pallas as pl
from jax.experimental.pallas import tpu as pltpu
from jax.sharding import PartitionSpec as P


LANES = 128
VMEM = pltpu.VMEM
BF16 = jnp.bfloat16
F32 = jnp.float32

QUARTERS = {
    "far": (3, 2, 1, 0),
    "out": (1, 3, 0, 2),
    "in": (2, 0, 3, 1),
    "own": (0, 1, 2, 3),
}
ORDER = ("far0", "own1", "far1", "out0", "out1", "in0", "in1", "own0")
WHOLE = "all"


def route(slot):
    turn, swap = QUARTERS[slot[:-1]], int(slot[-1])
    half = len(ORDER) // len(turn)
    return [turn[h // half] * half + (h % half ^ swap) for h in range(len(ORDER))]


def place(slot, size):
    if slot == WHOLE:
        return 0
    targets = route(slot)
    here = lax.axis_index("harm")
    start = jnp.int32(targets.index(0) * size)
    for spot in range(1, len(targets)):
        start = jnp.where(here == spot, targets.index(spot) * size, start)
    return pl.multiple_of(start, size)


def listed(*sets):
    arrays, maps = [], []
    for group in sets:
        found = {}
        for slot, (value, part) in group.items():
            spot = next((i for i, a in enumerate(arrays) if a is value), len(arrays))
            if spot == len(arrays):
                arrays.append(value)
            found[slot] = (spot, part)
        maps.append(found)
    return arrays, maps


def read(refs, entry):
    spot, part = entry
    return refs[spot][...] if part is None else refs[spot][part]


def call(body, outs, args, limit, scratch=()):
    spec = pl.BlockSpec(memory_space=VMEM)
    return pl.pallas_call(
        body,
        out_shape=outs,
        in_specs=[spec] * len(args),
        out_specs=jax.tree.map(lambda _: spec, outs),
        scratch_shapes=list(scratch),
        compiler_params=pltpu.CompilerParams(vmem_limit_bytes=limit << 20),
    )(*[pltpu.with_memory_space_constraint(a, VMEM) for a in args])


def product(matrix_ref, pieces):
    rows = matrix_ref.shape[1]
    part = jnp.zeros((rows, 2 * LANES), F32)
    by_re, by_im = part, part
    for slot, value in pieces.items():
        size = value.shape[1]
        cols = pl.ds(place(slot, size), size)
        both = jnp.concatenate([value[0], value[1]], axis=1)
        by_re += jnp.dot(matrix_ref[0, :, cols], both, preferred_element_type=F32)
        by_im += jnp.dot(matrix_ref[1, :, cols], both, preferred_element_type=F32)
    re = by_re[:, :LANES] - by_im[:, LANES:]
    im = by_re[:, LANES:] + by_im[:, :LANES]
    return re.astype(BF16), im.astype(BF16)


def propagate(matrix, group):
    arrays, (spots,) = listed(group)

    def body(matrix_ref, *refs):
        out_ref = refs[-1]
        re, im = product(matrix_ref, {slot: read(refs, e) for slot, e in spots.items()})
        out_ref[0] = re
        out_ref[1] = im

    rows = matrix.shape[1]
    return call(body, VMEM((2, rows, LANES), BF16), [matrix, *arrays], 8)


def one_hot(targets, first, count):
    index = lax.broadcasted_iota(jnp.int32, (count, targets.shape[1]), 0) + first
    return jnp.where(index == targets, 1.0, 0.0).astype(BF16)


def fill(whole, pieces):
    for slot, value in pieces.items():
        rows = pl.ds(place(slot, value.shape[1]), value.shape[1])
        whole[rows, :LANES] = value[0]
        whole[rows, LANES:] = value[1]


def bring(matrix, source, orders):
    args = [matrix, source, orders]

    def body(*refs):
        size = len(args)
        ins, outs, sems = refs[:size], refs[size : 2 * size], refs[-1]
        copies = [
            pltpu.make_async_copy(ins[i], outs[i], sems.at[i]) for i in range(size)
        ]
        for copy in copies:
            copy.start()
        for copy in copies:
            copy.wait()

    hbm = pl.BlockSpec(memory_space=pltpu.HBM)
    return pl.pallas_call(
        body,
        out_shape=[VMEM(a.shape, a.dtype) for a in args],
        in_specs=[hbm] * len(args),
        out_specs=[pl.BlockSpec(memory_space=VMEM)] * len(args),
        scratch_shapes=[pltpu.SemaphoreType.DMA((len(args),))],
        compiler_params=pltpu.CompilerParams(vmem_limit_bytes=1 << 20),
        name="bring",
    )(*[pltpu.with_memory_space_constraint(a, pltpu.HBM) for a in args])


def sort_fields(orders, low, high, split):
    harmonics = orders.shape[1]
    blocks = harmonics // LANES
    arrays, (low_spots, high_spots) = listed(low, high)

    def body(orders_ref, *refs):
        out_ref, whole = refs[-2:]
        lower = lax.axis_index("layer") < split
        pieces = {}
        for slot, entry in low_spots.items():
            pieces[slot] = read(refs, entry)
            if high_spots[slot] != entry:
                pieces[slot] = jnp.where(lower, pieces[slot], read(refs, high_spots[slot]))
        fill(whole, pieces)
        targets = orders_ref[...] ^ (LANES - 1)
        chunk = 4 * LANES

        def step(c, carry):
            picked = jnp.dot(
                one_hot(targets, c * chunk, chunk), whole[...], preferred_element_type=F32
            ).astype(BF16)
            for b in range(chunk // LANES):
                re = picked[b * LANES : (b + 1) * LANES, :LANES]
                im = picked[b * LANES : (b + 1) * LANES, LANES:]
                at = pl.multiple_of((c * (chunk // LANES) + b) * 2 * LANES, LANES)
                out_ref[:LANES, pl.ds(at, LANES)] = re
                out_ref[:LANES, pl.ds(at + LANES, LANES)] = -im
                out_ref[LANES:, pl.ds(at, LANES)] = im
                out_ref[LANES:, pl.ds(at + LANES, LANES)] = re
            return carry

        lax.fori_loop(0, harmonics // chunk, step, 0)

    return call(
        body,
        VMEM((2 * LANES, blocks * 2 * LANES), BF16),
        [orders, *arrays],
        24,
        [VMEM((harmonics, 2 * LANES), BF16)],
    )


def finish(matrix, orders, factors, sets, belows, band, scale):
    layers = len(sets)
    harmonics = orders.shape[1]
    rows = matrix.shape[1]
    blocks = harmonics // LANES
    bands = band // LANES
    strip = bands + 1
    arrays, maps = listed(*sets)

    def body(matrix_ref, orders_ref, factors_ref, *refs):
        set_refs, refs = refs[: len(arrays)], refs[len(arrays) :]
        below_refs, refs = refs[: layers - 1], refs[layers - 1 :]
        grad_ref, bottom_ref, whole, moved = refs
        layer = lax.axis_index("layer")
        last = {slot: read(set_refs, e) for slot, e in maps[0].items()}
        chosen = dict(last)
        for index in range(1, layers):
            for slot, entry in maps[index].items():
                chosen[slot] = jnp.where(layer == index, read(set_refs, entry), chosen[slot])
        fill(whole, chosen)
        re, im = product(matrix_ref, last)
        for index in range(1, layers):
            re = jnp.where(layer == index, below_refs[index - 1][0], re)
            im = jnp.where(layer == index, below_refs[index - 1][1], im)
        bottom_ref[0, 0] = re
        bottom_ref[0, 1] = im

        targets = orders_ref[...] + (harmonics - 1 - band * lax.axis_index("harm"))
        for c in range(blocks + bands):
            picked = jnp.dot(
                one_hot(targets, c * LANES, LANES), whole[...], preferred_element_type=F32
            ).astype(BF16)
            moved[:, c * 2 * LANES : (c + 1) * 2 * LANES] = picked
        width = 2 * LANES
        length = blocks * width
        parts = []
        for q in range(strip):
            parts.append(
                lax.dot_general(
                    factors_ref[...],
                    moved[:, q * width : q * width + length],
                    (((1,), (1,)), ((), ())),
                    preferred_element_type=F32,
                )
            )
        strips = jnp.concatenate(parts, axis=1)
        size = strip * LANES
        for part in range(2):
            skewed = pltpu.roll(
                strips[part * LANES : (part + 1) * LANES],
                size - (LANES - 1),
                1,
                stride=1,
                stride_axis=0,
            )
            total = jnp.sum(skewed[:, :band], axis=0, keepdims=True) * scale
            grad_ref[0, pl.ds(part, 1), :] = total

    outs = (
        jax.ShapeDtypeStruct((1, 2, band), F32),
        jax.ShapeDtypeStruct((1, 2, rows, LANES), BF16),
    )
    return call(
        body,
        outs,
        [matrix, orders, factors, *arrays, *belows],
        24,
        [
            VMEM((harmonics, 2 * LANES), BF16),
            VMEM((LANES, (blocks + bands) * 2 * LANES), BF16),
        ],
    )


def sweep(*args):
    layers, count = lax.axis_size("layer"), lax.axis_size("harm")
    if layers > 2 and count == len(ORDER) and args[0].shape[1] % LANES == 0:
        return direct_sweep(*args)
    return gather_sweep(*args)


def sizes(source, orders):
    harmonics = orders.shape[0]
    band = 2 * harmonics // lax.axis_size("harm")
    return band, 1.0 / math.sqrt(harmonics * source.shape[2])


def gather_sweep(source, transfer, fields, orders):
    layers, count = lax.axis_size("layer"), lax.axis_size("harm")
    band, scale = sizes(source, orders)

    def gathered(value):
        return {WHOLE: (lax.all_gather(value, "harm", axis=1, tiled=True), None)}

    matrix, _, table = bring(transfer[0], source, orders.reshape(1, -1))
    group = gathered(source)
    sets, belows = [group], []
    for layer in range(layers - 1, 0, -1):
        below = propagate(matrix, group)
        pairs = [(layer * count + h, (layer - 1) * count + h) for h in range(count)]
        group = gathered(lax.ppermute(below, ("layer", "harm"), pairs))
        sets.append(group)
        belows.append(below)
    held = gathered(fields[0])
    factors = sort_fields(table, held, held, layers)
    return finish(matrix, table, factors, sets[::-1], belows[::-1], band, scale)


def direct_sweep(source, transfer, fields, orders):
    layers, count = lax.axis_size("layer"), lax.axis_size("harm")
    band, scale = sizes(source, orders)
    top = layers - 1
    split = layers // 2

    def move(value, origin, target, slot):
        pairs = [(origin * count + h, target * count + t) for h, t in enumerate(route(slot))]
        return lax.ppermute(value, ("layer", "harm"), pairs)

    def among(value, members, slot):
        pairs = [
            (r * count + h, r * count + t) for r in members for h, t in enumerate(route(slot))
        ]
        return lax.ppermute(value, ("layer", "harm"), pairs)

    def along(pair, members):
        group = {"own0": (pair, 0), "own1": (pair, 1)}
        for name in ("far", "out", "in"):
            got = among(pair, members, name + "0")
            group[name + "0"] = (got, 0)
            group[name + "1"] = (got, 1)
        return group

    matrix, own, table = bring(transfer[0], source, orders.reshape(1, -1))
    group = {}
    for step, slot in enumerate(("far0", "far1", "out0", "out1")):
        group[slot] = (move(source, (step + 1) % top, top, slot), None)
    both = among(jnp.stack([fields[0], source]), range(layers), "own1")
    group["own1"] = (both, 1)
    got = move(jnp.stack([source, both[1]]), 0, top, "in0")
    group["in0"] = (got, 0)
    group["in1"] = (got, 1)
    group["own0"] = (own, None)
    pair = jnp.stack([fields[0], both[0]])
    low = along(pair, range(split))

    sets, belows = [group], []
    for layer in range(top, 0, -1):
        below = propagate(matrix, group)
        group = {}
        for slot in ORDER:
            group[slot] = (move(below, layer, layer - 1, slot), None)
        sets.append(group)
        belows.append(below)
        if layer == top - 1:
            held, _ = lax.optimization_barrier((pair, below))
            high = along(held, range(split, layers))
    for slot in ("own0", "own1"):
        low[slot] = high[slot]
    factors = sort_fields(table, low, high, split)
    return finish(matrix, table, factors, sets[::-1], belows[::-1], band, scale)


def solution(mesh):
    return jax.shard_map(
        sweep,
        mesh=mesh,
        in_specs=(
            P(None, "harm", None),
            P("layer", None, "harm", None),
            P("layer", None, "harm", None),
            P(),
        ),
        out_specs=(P("layer", None, "harm"), P("layer", None, "harm", None)),
        check_vma=False,
    )
```

profile of v0, /device:TPU:0, one launch (start us, length us, event | category | flops | bytes accessed | tf_op | source)
XLA Modules:
  0.0 102.7 jit_solution(13687770582886386067)
XLA Ops:
  0.6 1.0 pad_maximum_fusion
  1.6 3.1 %collective-permute-start = (bf16[2,2,256,128]{3,2,1,0:T(8,128)(2,1)S(1)}, bf16[2,2,256,128]{3,2,1,0:T(8,128)(2,1)S(1)}, u32[]{:S(2)}, u32[]{:S(2)}) collective-permute-start(bf16[2,2,256,128]{3,2,1,0:T(8,128)(2,1)S(1)} %pad_maximum_fusion), channel_id=1, source_target_pairs={{0,1},{1,0},{2,3},{3,2},{4,5},{5,4},{6,7},{7,6},{8,9},{9,8},{10,11... | collective-permute-start | bytes 786440 | tf_op jit(solution)/shard_map/ppermute | solution.py:303
  4.7 6.3 %collective-permute-done.refs_4_.refs_28_ = bf16[2,2,256,128]{3,2,1,0:T(8,128)(2,1)S(1)} collective-permute-done((bf16[2,2,256,128]{3,2,1,0:T(8,128)(2,1)S(1)}, bf16[2,2,256,128]{3,2,1,0:T(8,128)(2,1)S(1)}, u32[]{:S(2)}, u32[]{:S(2)}) %collective-permute-start) | collective-permute-done | bytes 262176 | tf_op jit(solution)/shard_map/ppermute | solution.py:303
  12.0 4.2 %collective-permute-start.5 = (bf16[2,2,256,128]{3,2,1,0:T(8,128)(2,1)S(1)}, bf16[2,2,256,128]{3,2,1,0:T(8,128)(2,1)S(1)}, u32[]{:S(2)}, u32[]{:S(2)}) collective-permute-start(bf16[2,2,256,128]{3,2,1,0:T(8,128)(2,1)S(1)} %pad_maximum_fusion.2), channel_id=1, source_target_pairs={{0,28},{1,29},{2,24},{3,25},{4,30},{5,31},{6,26},{7,27}} | collective-permute-start | bytes 786440 | tf_op jit(solution)/shard_map/ppermute | solution.py:297
  17.6 1.5 %collective-permute-start.3 = (bf16[2,256,128]{2,1,0:T(8,128)(2,1)}, bf16[2,256,128]{2,1,0:T(8,128)(2,1)S(1)}, u32[]{:S(2)}, u32[]{:S(2)}) collective-permute-start(bf16[2,256,128]{2,1,0:T(8,128)(2,1)} %refs_1_.1), channel_id=1, source_target_pairs={{0,26},{1,27},{2,30},{3,31},{4,24},{5,25},{6,28},{7,29}} | collective-permute-start | bytes 393224 | tf_op jit(solution)/shard_map/ppermute | solution.py:297
  19.8 1.6 %bring.1 = (bf16[2,256,2048]{2,1,0:T(8,128)(2,1)S(1)}, bf16[2,256,128]{2,1,0:T(8,128)(2,1)S(1)}, s32[1,2048]{1,0:T(1,128)S(1)}) custom-call(bf16[2,256,2048]{2,1,0:T(8,128)(2,1)} %bitcast.3, bf16[2,256,128]{2,1,0:T(8,128)(2,1)} %refs_1_.1, s32[1,2048]{1,0:T(1,128)} %bitcast.6), custom_call_target="tpu_custom_call" | custom-call | tf_op jit(solution)/shard_map/bring/pallas_call | solution.py:128
  21.4 3.1 %collective-permute-done.3.refs_2_.refs_26_ = bf16[2,256,128]{2,1,0:T(8,128)(2,1)S(1)} collective-permute-done((bf16[2,256,128]{2,1,0:T(8,128)(2,1)}, bf16[2,256,128]{2,1,0:T(8,128)(2,1)S(1)}, u32[]{:S(2)}, u32[]{:S(2)}) %collective-permute-start.3) | collective-permute-done | bytes 131104 | tf_op jit(solution)/shard_map/ppermute | solution.py:297
  28.0 2.0 %collective-permute-start.14 = (bf16[2,2,256,128]{3,2,1,0:T(8,128)(2,1)S(1)}, bf16[2,2,256,128]{3,2,1,0:T(8,128)(2,1)S(1)}, u32[]{:S(2)}, u32[]{:S(2)}) collective-permute-start(bf16[2,2,256,128]{3,2,1,0:T(8,128)(2,1)S(1)} %pad_maximum_fusion.1.refs_0_), channel_id=1, source_target_pairs={{0,6},{1,7},{2,4},{3,5},{4,2},{5,3},{6,0},{7,1},{8,14},{9,15},{10,... | collective-permute-start | bytes 786440 | tf_op jit(solution)/shard_map/ppermute | solution.py:303
  36.2 4.7 %collective-permute-done.14.refs_1_ = bf16[2,2,256,128]{3,2,1,0:T(8,128)(2,1)S(1)} collective-permute-done((bf16[2,2,256,128]{3,2,1,0:T(8,128)(2,1)S(1)}, bf16[2,2,256,128]{3,2,1,0:T(8,128)(2,1)S(1)}, u32[]{:S(2)}, u32[]{:S(2)}) %collective-permute-start.14) | collective-permute-done | bytes 262176 | tf_op jit(solution)/shard_map/ppermute | solution.py:303
  43.6 7.1 %collective-permute-start.15 = (bf16[2,2,256,128]{3,2,1,0:T(8,128)(2,1)S(1)}, bf16[2,2,256,128]{3,2,1,0:T(8,128)(2,1)S(1)}, u32[]{:S(2)}, u32[]{:S(2)}) collective-permute-start(bf16[2,2,256,128]{3,2,1,0:T(8,128)(2,1)S(1)} %pad_maximum_fusion.1.refs_0_), channel_id=1, source_target_pairs={{0,2},{1,3},{2,6},{3,7},{4,0},{5,1},{6,4},{7,5},{8,10},{9,11},{10,... | collective-permute-start | bytes 786440 | tf_op jit(solution)/shard_map/ppermute | solution.py:303
  50.7 1.9 %collective-permute-start.16 = (bf16[2,2,256,128]{3,2,1,0:T(8,128)(2,1)S(1)}, bf16[2,2,256,128]{3,2,1,0:T(8,128)(2,1)S(1)}, u32[]{:S(2)}, u32[]{:S(2)}) collective-permute-start(bf16[2,2,256,128]{3,2,1,0:T(8,128)(2,1)S(1)} %pad_maximum_fusion.1.refs_0_), channel_id=1, source_target_pairs={{0,4},{1,5},{2,0},{3,1},{4,6},{5,7},{6,2},{7,3},{8,12},{9,13},{10,... | collective-permute-start | bytes 786440 | tf_op jit(solution)/shard_map/ppermute | solution.py:303
  55.4 1.3 %collective-permute-start.28 = (bf16[2,256,128]{2,1,0:T(8,128)(2,1)S(1)}, bf16[2,256,128]{2,1,0:T(8,128)(2,1)S(1)}, u32[]{:S(2)}, u32[]{:S(2)}) collective-permute-start(bf16[2,256,128]{2,1,0:T(8,128)(2,1)S(1)} %shard_map.62.refs_31_), channel_id=1, source_target_pairs={{8,6},{9,7},{10,4},{11,5},{12,2},{13,3},{14,0},{15,1}} | collective-permute-start | bytes 393224 | tf_op jit(solution)/shard_map/ppermute | solution.py:297
  56.7 2.2 %collective-permute-done.16.refs_3_ = bf16[2,2,256,128]{3,2,1,0:T(8,128)(2,1)S(1)} collective-permute-done((bf16[2,2,256,128]{3,2,1,0:T(8,128)(2,1)S(1)}, bf16[2,2,256,128]{3,2,1,0:T(8,128)(2,1)S(1)}, u32[]{:S(2)}, u32[]{:S(2)}) %collective-permute-start.16) | collective-permute-done | bytes 262176 | tf_op jit(solution)/shard_map/ppermute | solution.py:303
  58.9 1.3 %collective-permute-start.29 = (bf16[2,256,128]{2,1,0:T(8,128)(2,1)S(1)}, bf16[2,256,128]{2,1,0:T(8,128)(2,1)S(1)}, u32[]{:S(2)}, u32[]{:S(2)}) collective-permute-start(bf16[2,256,128]{2,1,0:T(8,128)(2,1)S(1)} %shard_map.62.refs_31_), channel_id=1, source_target_pairs={{8,1},{9,0},{10,3},{11,2},{12,5},{13,4},{14,7},{15,6}} | collective-permute-start | bytes 393224 | tf_op jit(solution)/shard_map/ppermute | solution.py:297
  60.2 1.3 %collective-permute-start.30 = (bf16[2,256,128]{2,1,0:T(8,128)(2,1)S(1)}, bf16[2,256,128]{2,1,0:T(8,128)(2,1)S(1)}, u32[]{:S(2)}, u32[]{:S(2)}) collective-permute-start(bf16[2,256,128]{2,1,0:T(8,128)(2,1)S(1)} %shard_map.62.refs_31_), channel_id=1, source_target_pairs={{8,7},{9,6},{10,5},{11,4},{12,3},{13,2},{14,1},{15,0}} | collective-permute-start | bytes 393224 | tf_op jit(solution)/shard_map/ppermute | solution.py:297
  61.5 1.3 %collective-permute-start.31 = (bf16[2,256,128]{2,1,0:T(8,128)(2,1)S(1)}, bf16[2,256,128]{2,1,0:T(8,128)(2,1)S(1)}, u32[]{:S(2)}, u32[]{:S(2)}) collective-permute-start(bf16[2,256,128]{2,1,0:T(8,128)(2,1)S(1)} %shard_map.62.refs_31_), channel_id=1, source_target_pairs={{8,2},{9,3},{10,6},{11,7},{12,0},{13,1},{14,4},{15,5}} | collective-permute-start | bytes 393224 | tf_op jit(solution)/shard_map/ppermute | solution.py:297
  62.9 1.3 %collective-permute-start.32 = (bf16[2,256,128]{2,1,0:T(8,128)(2,1)S(1)}, bf16[2,256,128]{2,1,0:T(8,128)(2,1)S(1)}, u32[]{:S(2)}, u32[]{:S(2)}) collective-permute-start(bf16[2,256,128]{2,1,0:T(8,128)(2,1)S(1)} %shard_map.62.refs_31_), channel_id=1, source_target_pairs={{8,3},{9,2},{10,7},{11,6},{12,1},{13,0},{14,5},{15,4}} | collective-permute-start | bytes 393224 | tf_op jit(solution)/shard_map/ppermute | solution.py:297
  64.2 21.2 %collective-permute-done.28.refs_0_ = bf16[2,256,128]{2,1,0:T(8,128)(2,1)S(1)} collective-permute-done((bf16[2,256,128]{2,1,0:T(8,128)(2,1)S(1)}, bf16[2,256,128]{2,1,0:T(8,128)(2,1)S(1)}, u32[]{:S(2)}, u32[]{:S(2)}) %collective-permute-start.28) | collective-permute-done | bytes 131104 | tf_op jit(solution)/shard_map/ppermute | solution.py:297
  85.4 1.3 %collective-permute-start.33 = (bf16[2,256,128]{2,1,0:T(8,128)(2,1)S(1)}, bf16[2,256,128]{2,1,0:T(8,128)(2,1)S(1)}, u32[]{:S(2)}, u32[]{:S(2)}) collective-permute-start(bf16[2,256,128]{2,1,0:T(8,128)(2,1)S(1)} %shard_map.62.refs_31_), channel_id=1, source_target_pairs={{8,4},{9,5},{10,0},{11,1},{12,6},{13,7},{14,2},{15,3}} | collective-permute-start | bytes 393224 | tf_op jit(solution)/shard_map/ppermute | solution.py:297
  86.7 1.3 %collective-permute-start.34 = (bf16[2,256,128]{2,1,0:T(8,128)(2,1)S(1)}, bf16[2,256,128]{2,1,0:T(8,128)(2,1)S(1)}, u32[]{:S(2)}, u32[]{:S(2)}) collective-permute-start(bf16[2,256,128]{2,1,0:T(8,128)(2,1)S(1)} %shard_map.62.refs_31_), channel_id=1, source_target_pairs={{8,5},{9,4},{10,1},{11,0},{12,7},{13,6},{14,3},{15,2}} | collective-permute-start | bytes 393224 | tf_op jit(solution)/shard_map/ppermute | solution.py:297
  88.0 2.0 %collective-permute-done.30.refs_2_ = bf16[2,256,128]{2,1,0:T(8,128)(2,1)S(1)} collective-permute-done((bf16[2,256,128]{2,1,0:T(8,128)(2,1)S(1)}, bf16[2,256,128]{2,1,0:T(8,128)(2,1)S(1)}, u32[]{:S(2)}, u32[]{:S(2)}) %collective-permute-start.30) | collective-permute-done | bytes 131104 | tf_op jit(solution)/shard_map/ppermute | solution.py:297
  89.9 1.3 %collective-permute-start.35 = (bf16[2,256,128]{2,1,0:T(8,128)(2,1)S(1)}, bf16[2,256,128]{2,1,0:T(8,128)(2,1)S(1)}, u32[]{:S(2)}, u32[]{:S(2)}) collective-permute-start(bf16[2,256,128]{2,1,0:T(8,128)(2,1)S(1)} %shard_map.62.refs_31_), channel_id=1, source_target_pairs={{8,0},{9,1},{10,2},{11,3},{12,4},{13,5},{14,6},{15,7}} | collective-permute-start | bytes 393224 | tf_op jit(solution)/shard_map/ppermute | solution.py:297
  91.2 3.3 %shard_map.61.factors_ref = bf16[256,4096]{1,0:T(8,128)(2,1)S(1)} custom-call(s32[1,2048]{1,0:T(1,128)S(1)} %get-tuple-element.7.orders_ref, bf16[2,2,256,128]{3,2,1,0:T(8,128)(2,1)S(1)} %pad_maximum_fusion.1.refs_0_, bf16[2,2,256,128]{3,2,1,0:T(8,128)(2,1)S(1)} %collective-permute-done.14.refs_1_, ...), custom_call_target="tpu_custom_call" | custom-call | tf_op jit(solution)/shard_map/pallas_call | solution.py:63
  95.2 7.5 %shard_map.63 = (f32[1,2,512]{2,1,0:T(2,128)}, bf16[1,2,256,128]{3,2,1,0:T(8,128)(2,1)}) custom-call(bf16[2,256,2048]{2,1,0:T(8,128)(2,1)S(1)} %get-tuple-element.6.matrix_ref, s32[1,2048]{1,0:T(1,128)S(1)} %get-tuple-element.7.orders_ref, bf16[256,4096]{1,0:T(8,128)(2,1)S(1)} %shard_map.61.factors_ref, ...), custom_call_target="tpu_custom_call" | custom-call | tf_op jit(solution)/shard_map/pallas_call | solution.py:63
  (60 shorter events, 18.6 us)
Async XLA Ops:
  1.6 9.4 %collective-permute-start = (bf16[2,2,256,128]{3,2,1,0:T(8,128)(2,1)S(1)}, bf16[2,2,256,128]{3,2,1,0:T(8,128)(2,1)S(1)}, u32[]{:S(2)}, u32[]{:S(2)}) collective-permute-start(bf16[2,2,256,128]{3,2,1,0:T(8,128)(2,1)S(1)} %pad_maximum_fusion), channel_id=1, source_target_pairs={{0,1},{1,0},{2,3},{3,2},{4,5},{5,4},{6,7},{7,6},{8,9},{9,8},{10,11... | collective-permute-start | bytes 786440 | tf_op jit(solution)/shard_map/ppermute | solution.py:303
  12.0 12.5 %collective-permute-start.5 = (bf16[2,2,256,128]{3,2,1,0:T(8,128)(2,1)S(1)}, bf16[2,2,256,128]{3,2,1,0:T(8,128)(2,1)S(1)}, u32[]{:S(2)}, u32[]{:S(2)}) collective-permute-start(bf16[2,2,256,128]{3,2,1,0:T(8,128)(2,1)S(1)} %pad_maximum_fusion.2), channel_id=1, source_target_pairs={{0,28},{1,29},{2,24},{3,25},{4,30},{5,31},{6,26},{7,27}} | collective-permute-start | bytes 786440 | tf_op jit(solution)/shard_map/ppermute | solution.py:297
  17.6 6.9 %collective-permute-start.3 = (bf16[2,256,128]{2,1,0:T(8,128)(2,1)}, bf16[2,256,128]{2,1,0:T(8,128)(2,1)S(1)}, u32[]{:S(2)}, u32[]{:S(2)}) collective-permute-start(bf16[2,256,128]{2,1,0:T(8,128)(2,1)} %refs_1_.1), channel_id=1, source_target_pairs={{0,26},{1,27},{2,30},{3,31},{4,24},{5,25},{6,28},{7,29}} | collective-permute-start | bytes 393224 | tf_op jit(solution)/shard_map/ppermute | solution.py:297
  28.0 12.9 %collective-permute-start.14 = (bf16[2,2,256,128]{3,2,1,0:T(8,128)(2,1)S(1)}, bf16[2,2,256,128]{3,2,1,0:T(8,128)(2,1)S(1)}, u32[]{:S(2)}, u32[]{:S(2)}) collective-permute-start(bf16[2,2,256,128]{3,2,1,0:T(8,128)(2,1)S(1)} %pad_maximum_fusion.1.refs_0_), channel_id=1, source_target_pairs={{0,6},{1,7},{2,4},{3,5},{4,2},{5,3},{6,0},{7,1},{8,14},{9,15},{10,... | collective-permute-start | bytes 786440 | tf_op jit(solution)/shard_map/ppermute | solution.py:303
  33.4 8.1 %collective-permute-start.20 = (bf16[2,256,128]{2,1,0:T(8,128)(2,1)S(1)}, bf16[2,256,128]{2,1,0:T(8,128)(2,1)S(1)}, u32[]{:S(2)}, u32[]{:S(2)}) collective-permute-start(bf16[2,256,128]{2,1,0:T(8,128)(2,1)S(1)} %shard_map.60.refs_32_), channel_id=1, source_target_pairs={{16,14},{17,15},{18,12},{19,13},{20,10},{21,11},{22,8},{23,9}} | collective-permute-start | bytes 393224 | tf_op jit(solution)/shard_map/ppermute | solution.py:297
  34.1 8.1 %collective-permute-start.21 = (bf16[2,256,128]{2,1,0:T(8,128)(2,1)S(1)}, bf16[2,256,128]{2,1,0:T(8,128)(2,1)S(1)}, u32[]{:S(2)}, u32[]{:S(2)}) collective-permute-start(bf16[2,256,128]{2,1,0:T(8,128)(2,1)S(1)} %shard_map.60.refs_32_), channel_id=1, source_target_pairs={{16,9},{17,8},{18,11},{19,10},{20,13},{21,12},{22,15},{23,14}} | collective-permute-start | bytes 393224 | tf_op jit(solution)/shard_map/ppermute | solution.py:297
  34.8 8.1 %collective-permute-start.22 = (bf16[2,256,128]{2,1,0:T(8,128)(2,1)S(1)}, bf16[2,256,128]{2,1,0:T(8,128)(2,1)S(1)}, u32[]{:S(2)}, u32[]{:S(2)}) collective-permute-start(bf16[2,256,128]{2,1,0:T(8,128)(2,1)S(1)} %shard_map.60.refs_32_), channel_id=1, source_target_pairs={{16,15},{17,14},{18,13},{19,12},{20,11},{21,10},{22,9},{23,8}} | collective-permute-start | bytes 393224 | tf_op jit(solution)/shard_map/ppermute | solution.py:297
  35.5 8.1 %collective-permute-start.23 = (bf16[2,256,128]{2,1,0:T(8,128)(2,1)S(1)}, bf16[2,256,128]{2,1,0:T(8,128)(2,1)S(1)}, u32[]{:S(2)}, u32[]{:S(2)}) collective-permute-start(bf16[2,256,128]{2,1,0:T(8,128)(2,1)S(1)} %shard_map.60.refs_32_), channel_id=1, source_target_pairs={{16,10},{17,11},{18,14},{19,15},{20,8},{21,9},{22,12},{23,13}} | collective-permute-start | bytes 393224 | tf_op jit(solution)/shard_map/ppermute | solution.py:297
  40.8 9.8 %collective-permute-start.24 = (bf16[2,256,128]{2,1,0:T(8,128)(2,1)S(1)}, bf16[2,256,128]{2,1,0:T(8,128)(2,1)S(1)}, u32[]{:S(2)}, u32[]{:S(2)}) collective-permute-start(bf16[2,256,128]{2,1,0:T(8,128)(2,1)S(1)} %shard_map.60.refs_32_), channel_id=1, source_target_pairs={{16,11},{17,10},{18,15},{19,14},{20,9},{21,8},{22,13},{23,12}} | collective-permute-start | bytes 393224 | tf_op jit(solution)/shard_map/ppermute | solution.py:297
  41.5 11.1 %collective-permute-start.25 = (bf16[2,256,128]{2,1,0:T(8,128)(2,1)S(1)}, bf16[2,256,128]{2,1,0:T(8,128)(2,1)S(1)}, u32[]{:S(2)}, u32[]{:S(2)}) collective-permute-start(bf16[2,256,128]{2,1,0:T(8,128)(2,1)S(1)} %shard_map.60.refs_32_), channel_id=1, source_target_pairs={{16,12},{17,13},{18,8},{19,9},{20,14},{21,15},{22,10},{23,11}} | collective-permute-start | bytes 393224 | tf_op jit(solution)/shard_map/ppermute | solution.py:297
  42.2 11.1 %collective-permute-start.26 = (bf16[2,256,128]{2,1,0:T(8,128)(2,1)S(1)}, bf16[2,256,128]{2,1,0:T(8,128)(2,1)S(1)}, u32[]{:S(2)}, u32[]{:S(2)}) collective-permute-start(bf16[2,256,128]{2,1,0:T(8,128)(2,1)S(1)} %shard_map.60.refs_32_), channel_id=1, source_target_pairs={{16,13},{17,12},{18,9},{19,8},{20,15},{21,14},{22,11},{23,10}} | collective-permute-start | bytes 393224 | tf_op jit(solution)/shard_map/ppermute | solution.py:297
  42.9 11.1 %collective-permute-start.27 = (bf16[2,256,128]{2,1,0:T(8,128)(2,1)S(1)}, bf16[2,256,128]{2,1,0:T(8,128)(2,1)S(1)}, u32[]{:S(2)}, u32[]{:S(2)}) collective-permute-start(bf16[2,256,128]{2,1,0:T(8,128)(2,1)S(1)} %shard_map.60.refs_32_), channel_id=1, source_target_pairs={{16,8},{17,9},{18,10},{19,11},{20,12},{21,13},{22,14},{23,15}} | collective-permute-start | bytes 393224 | tf_op jit(solution)/shard_map/ppermute | solution.py:297
  43.6 11.8 %collective-permute-start.15 = (bf16[2,2,256,128]{3,2,1,0:T(8,128)(2,1)S(1)}, bf16[2,2,256,128]{3,2,1,0:T(8,128)(2,1)S(1)}, u32[]{:S(2)}, u32[]{:S(2)}) collective-permute-start(bf16[2,2,256,128]{3,2,1,0:T(8,128)(2,1)S(1)} %pad_maximum_fusion.1.refs_0_), channel_id=1, source_target_pairs={{0,2},{1,3},{2,6},{3,7},{4,0},{5,1},{6,4},{7,5},{8,10},{9,11},{10,... | collective-permute-start | bytes 786440 | tf_op jit(solution)/shard_map/ppermute | solution.py:303
  50.7 8.3 %collective-permute-start.16 = (bf16[2,2,256,128]{3,2,1,0:T(8,128)(2,1)S(1)}, bf16[2,2,256,128]{3,2,1,0:T(8,128)(2,1)S(1)}, u32[]{:S(2)}, u32[]{:S(2)}) collective-permute-start(bf16[2,2,256,128]{3,2,1,0:T(8,128)(2,1)S(1)} %pad_maximum_fusion.1.refs_0_), channel_id=1, source_target_pairs={{0,4},{1,5},{2,0},{3,1},{4,6},{5,7},{6,2},{7,3},{8,12},{9,13},{10,... | collective-permute-start | bytes 786440 | tf_op jit(solution)/shard_map/ppermute | solution.py:303
  52.6 7.6 %collective-permute-start.17 = (bf16[2,2,256,128]{3,2,1,0:T(8,128)(2,1)S(1)}, bf16[2,2,256,128]{3,2,1,0:T(8,128)(2,1)S(1)}, u32[]{:S(2)}, u32[]{:S(2)}) collective-permute-start(bf16[2,2,256,128]{3,2,1,0:T(8,128)(2,1)S(1)} %pad_maximum_fusion.1.refs_0_), channel_id=1, source_target_pairs={{16,22},{17,23},{18,20},{19,21},{20,18},{21,19},{22,16},{23,17},{2... | collective-permute-start | bytes 786440 | tf_op jit(solution)/shard_map/ppermute | solution.py:303
  53.3 8.2 %collective-permute-start.18 = (bf16[2,2,256,128]{3,2,1,0:T(8,128)(2,1)S(1)}, bf16[2,2,256,128]{3,2,1,0:T(8,128)(2,1)S(1)}, u32[]{:S(2)}, u32[]{:S(2)}) collective-permute-start(bf16[2,2,256,128]{3,2,1,0:T(8,128)(2,1)S(1)} %pad_maximum_fusion.1.refs_0_), channel_id=1, source_target_pairs={{16,18},{17,19},{18,22},{19,23},{20,16},{21,17},{22,20},{23,21},{2... | collective-permute-start | bytes 786440 | tf_op jit(solution)/shard_map/ppermute | solution.py:303
  54.0 8.8 %collective-permute-start.19 = (bf16[2,2,256,128]{3,2,1,0:T(8,128)(2,1)S(1)}, bf16[2,2,256,128]{3,2,1,0:T(8,128)(2,1)S(1)}, u32[]{:S(2)}, u32[]{:S(2)}) collective-permute-start(bf16[2,2,256,128]{3,2,1,0:T(8,128)(2,1)S(1)} %pad_maximum_fusion.1.refs_0_), channel_id=1, source_target_pairs={{16,20},{17,21},{18,16},{19,17},{20,22},{21,23},{22,18},{23,19},{2... | collective-permute-start | bytes 786440 | tf_op jit(solution)/shard_map/ppermute | solution.py:303
  55.4 29.9 %collective-permute-start.28 = (bf16[2,256,128]{2,1,0:T(8,128)(2,1)S(1)}, bf16[2,256,128]{2,1,0:T(8,128)(2,1)S(1)}, u32[]{:S(2)}, u32[]{:S(2)}) collective-permute-start(bf16[2,256,128]{2,1,0:T(8,128)(2,1)S(1)} %shard_map.62.refs_31_), channel_id=1, source_target_pairs={{8,6},{9,7},{10,4},{11,5},{12,2},{13,3},{14,0},{15,1}} | collective-permute-start | bytes 393224 | tf_op jit(solution)/shard_map/ppermute | solution.py:297
  58.9 27.7 %collective-permute-start.29 = (bf16[2,256,128]{2,1,0:T(8,128)(2,1)S(1)}, bf16[2,256,128]{2,1,0:T(8,128)(2,1)S(1)}, u32[]{:S(2)}, u32[]{:S(2)}) collective-permute-start(bf16[2,256,128]{2,1,0:T(8,128)(2,1)S(1)} %shard_map.62.refs_31_), channel_id=1, source_target_pairs={{8,1},{9,0},{10,3},{11,2},{12,5},{13,4},{14,7},{15,6}} | collective-permute-start | bytes 393224 | tf_op jit(solution)/shard_map/ppermute | solution.py:297
  60.2 29.7 %collective-permute-start.30 = (bf16[2,256,128]{2,1,0:T(8,128)(2,1)S(1)}, bf16[2,256,128]{2,1,0:T(8,128)(2,1)S(1)}, u32[]{:S(2)}, u32[]{:S(2)}) collective-permute-start(bf16[2,256,128]{2,1,0:T(8,128)(2,1)S(1)} %shard_map.62.refs_31_), channel_id=1, source_target_pairs={{8,7},{9,6},{10,5},{11,4},{12,3},{13,2},{14,1},{15,0}} | collective-permute-start | bytes 393224 | tf_op jit(solution)/shard_map/ppermute | solution.py:297
  61.5 32.9 %collective-permute-start.31 = (bf16[2,256,128]{2,1,0:T(8,128)(2,1)S(1)}, bf16[2,256,128]{2,1,0:T(8,128)(2,1)S(1)}, u32[]{:S(2)}, u32[]{:S(2)}) collective-permute-start(bf16[2,256,128]{2,1,0:T(8,128)(2,1)S(1)} %shard_map.62.refs_31_), channel_id=1, source_target_pairs={{8,2},{9,3},{10,6},{11,7},{12,0},{13,1},{14,4},{15,5}} | collective-permute-start | bytes 393224 | tf_op jit(solution)/shard_map/ppermute | solution.py:297
  62.9 31.6 %collective-permute-start.32 = (bf16[2,256,128]{2,1,0:T(8,128)(2,1)S(1)}, bf16[2,256,128]{2,1,0:T(8,128)(2,1)S(1)}, u32[]{:S(2)}, u32[]{:S(2)}) collective-permute-start(bf16[2,256,128]{2,1,0:T(8,128)(2,1)S(1)} %shard_map.62.refs_31_), channel_id=1, source_target_pairs={{8,3},{9,2},{10,7},{11,6},{12,1},{13,0},{14,5},{15,4}} | collective-permute-start | bytes 393224 | tf_op jit(solution)/shard_map/ppermute | solution.py:297
  85.4 9.3 %collective-permute-start.33 = (bf16[2,256,128]{2,1,0:T(8,128)(2,1)S(1)}, bf16[2,256,128]{2,1,0:T(8,128)(2,1)S(1)}, u32[]{:S(2)}, u32[]{:S(2)}) collective-permute-start(bf16[2,256,128]{2,1,0:T(8,128)(2,1)S(1)} %shard_map.62.refs_31_), channel_id=1, source_target_pairs={{8,4},{9,5},{10,0},{11,1},{12,6},{13,7},{14,2},{15,3}} | collective-permute-start | bytes 393224 | tf_op jit(solution)/shard_map/ppermute | solution.py:297
  86.7 8.5 %collective-permute-start.34 = (bf16[2,256,128]{2,1,0:T(8,128)(2,1)S(1)}, bf16[2,256,128]{2,1,0:T(8,128)(2,1)S(1)}, u32[]{:S(2)}, u32[]{:S(2)}) collective-permute-start(bf16[2,256,128]{2,1,0:T(8,128)(2,1)S(1)} %shard_map.62.refs_31_), channel_id=1, source_target_pairs={{8,5},{9,4},{10,1},{11,0},{12,7},{13,6},{14,3},{15,2}} | collective-permute-start | bytes 393224 | tf_op jit(solution)/shard_map/ppermute | solution.py:297
  (13 other events, 52.9 us)
where the time goes:
time: 105 us; the launch traced here: 103 us
  starting transfers between devices  44.8 us (43%)
  waiting for transfers between devices  40.2 us (38%)
  Pallas kernels  14.5 us (14%)
  other arithmetic  1.96 us (2%)
  between operations  1.18 us (1%)
    ppermute x29, starting transfers between devices, move(): return lax.ppermute(value, ('layer', 'harm'), pairs)  28.8 us
    ppermute x29, waiting for transfers between devices, move(): return lax.ppermute(value, ('layer', 'harm'), pairs)  27 us
    ppermute x7, starting transfers between devices, among(): return lax.ppermute(value, ('layer', 'harm'), pairs)  16.1 us
    ppermute x7, waiting for transfers between devices, among(): return lax.ppermute(value, ('layer', 'harm'), pairs)  13.2 us
    pallas_call x5, Pallas kernels, call(): pl.pallas_call(body, out_shape=outs, in_specs=[spec] * len(args), out_spe...  12.9 us
  transfers between devices with their start and end apart: 36, of which 8 were waited for; matrix products, arithmetic and copies ran while one was open for 0% of the time, Pallas kernels for 6%

commit v1 on v0

--- a/solution.py
+++ b/solution.py
@@ -20,6 +20,7 @@
     "own": (0, 1, 2, 3),
 }
 ORDER = ("far0", "own1", "far1", "out0", "out1", "in0", "in1", "own0")
+TURNS = ("far", "out", "in")
 WHOLE = "all"
 
 
@@ -136,20 +137,14 @@
     )(*[pltpu.with_memory_space_constraint(a, pltpu.HBM) for a in args])
 
 
-def sort_fields(orders, low, high, split):
+def sort_fields(orders, held):
     harmonics = orders.shape[1]
     blocks = harmonics // LANES
-    arrays, (low_spots, high_spots) = listed(low, high)
+    arrays, (spots,) = listed(held)
 
     def body(orders_ref, *refs):
         out_ref, whole = refs[-2:]
-        lower = lax.axis_index("layer") < split
-        pieces = {}
-        for slot, entry in low_spots.items():
-            pieces[slot] = read(refs, entry)
-            if high_spots[slot] != entry:
-                pieces[slot] = jnp.where(lower, pieces[slot], read(refs, high_spots[slot]))
-        fill(whole, pieces)
+        fill(whole, {slot: read(refs, e) for slot, e in spots.items()})
         targets = orders_ref[...] ^ (LANES - 1)
         chunk = 4 * LANES
 
@@ -281,8 +276,7 @@
         group = gathered(lax.ppermute(below, ("layer", "harm"), pairs))
         sets.append(group)
         belows.append(below)
-    held = gathered(fields[0])
-    factors = sort_fields(table, held, held, layers)
+    factors = sort_fields(table, gathered(fields[0]))
     return finish(matrix, table, factors, sets[::-1], belows[::-1], band, scale)
 
 
@@ -302,26 +296,12 @@
         ]
         return lax.ppermute(value, ("layer", "harm"), pairs)
 
-    def along(pair, members):
-        group = {"own0": (pair, 0), "own1": (pair, 1)}
-        for name in ("far", "out", "in"):
-            got = among(pair, members, name + "0")
-            group[name + "0"] = (got, 0)
-            group[name + "1"] = (got, 1)
-        return group
-
     matrix, own, table = bring(transfer[0], source, orders.reshape(1, -1))
-    group = {}
-    for step, slot in enumerate(("far0", "far1", "out0", "out1")):
-        group[slot] = (move(source, (step + 1) % top, top, slot), None)
-    both = among(jnp.stack([fields[0], source]), range(layers), "own1")
-    group["own1"] = (both, 1)
-    got = move(jnp.stack([source, both[1]]), 0, top, "in0")
-    group["in0"] = (got, 0)
-    group["in1"] = (got, 1)
-    group["own0"] = (own, None)
-    pair = jnp.stack([fields[0], both[0]])
-    low = along(pair, range(split))
+    group = {"own0": (own, None)}
+    for slot in ORDER[:-1]:
+        origin = top - 1 if slot[-1] == "1" and slot != "own1" else len(group) % split
+        group[slot] = (move(source, origin, top, slot), None)
+    along = [among(fields[0], range(layers), turn + "0") for turn in TURNS]
 
     sets, belows = [group], []
     for layer in range(top, 0, -1):
@@ -332,11 +312,14 @@
         sets.append(group)
         belows.append(below)
         if layer == top - 1:
-            held, _ = lax.optimization_barrier((pair, below))
-            high = along(held, range(split, layers))
-    for slot in ("own0", "own1"):
-        low[slot] = high[slot]
-    factors = sort_fields(table, low, high, split)
+            along, _ = lax.optimization_barrier((along, below))
+            mine = jnp.stack([*along, fields[0]])
+            beside = among(mine, range(layers), "own1")
+    held = {}
+    for part, turn in enumerate((*TURNS, "own")):
+        held[turn + "0"] = (mine, part)
+        held[turn + "1"] = (beside, part)
+    factors = sort_fields(table, held)
     return finish(matrix, table, factors, sets[::-1], belows[::-1], band, scale)
 
 

time: 105 us -> 98.2 us (0.935)
  the two profiles are of different devices: /device:TPU:0 before, /device:TPU:1 now
where the time goes in v1:
time: 98.2 us; the launch traced here: 97.6 us
  starting transfers between devices  45.7 us (47%)
  waiting for transfers between devices  36.2 us (37%)
  Pallas kernels  14.5 us (15%)
  between operations  1.13 us (1%)
    ppermute x31, starting transfers between devices, move(): return lax.ppermute(value, ('layer', 'harm'), pairs)  42 us
    ppermute x31, waiting for transfers between devices, move(): return lax.ppermute(value, ('layer', 'harm'), pairs)  31.5 us
    pallas_call x5, Pallas kernels, call(): pl.pallas_call(body, out_shape=outs, in_specs=[spec] * len(args), out_spe...  12.9 us
    ppermute x4, waiting for transfers between devices, among(): return lax.ppermute(value, ('layer', 'harm'), pairs)  4.7 us
    ppermute x4, starting transfers between devices, among(): return lax.ppermute(value, ('layer', 'harm'), pairs)  3.69 us
  transfers between devices with their start and end apart: 35, of which 8 were waited for; matrix products, arithmetic and copies ran while one was open for 0% of the time, Pallas kernels for 6%

profile of v1, /device:TPU:1, one launch (start us, length us, event | category | flops | bytes accessed | tf_op | source)
XLA Modules:
  0.0 97.6 jit_solution(3359071757132757396)
XLA Ops:
  0.6 7.0 %collective-permute-start.3 = (bf16[2,256,128]{2,1,0:T(8,128)(2,1)}, bf16[2,256,128]{2,1,0:T(8,128)(2,1)S(1)}, u32[]{:S(2)}, u32[]{:S(2)}) collective-permute-start(bf16[2,256,128]{2,1,0:T(8,128)(2,1)} %refs_1_.1), channel_id=1, source_target_pairs={{8,30},{9,31},{10,28},{11,29},{12,26},{13,27},{14,24},{15,25}} | collective-permute-start | bytes 393224 | tf_op jit(solution)/shard_map/ppermute | solution.py:291
  11.7 1.6 %bring.1 = (bf16[2,256,2048]{2,1,0:T(8,128)(2,1)S(1)}, bf16[2,256,128]{2,1,0:T(8,128)(2,1)S(1)}, s32[1,2048]{1,0:T(1,128)S(1)}) custom-call(bf16[2,256,2048]{2,1,0:T(8,128)(2,1)} %bitcast.6, bf16[2,256,128]{2,1,0:T(8,128)(2,1)} %refs_1_.1, s32[1,2048]{1,0:T(1,128)} %bitcast.13), custom_call_target="tpu_custom_call" | custom-call | tf_op jit(solution)/shard_map/bring/pallas_call | solution.py:129
  20.0 2.0 %collective-permute-start.2 = (bf16[2,256,128]{2,1,0:T(8,128)(2,1)S(1)}, bf16[2,256,128]{2,1,0:T(8,128)(2,1)S(1)}, u32[]{:S(2)}, u32[]{:S(2)}) collective-permute-start(bf16[2,256,128]{2,1,0:T(8,128)(2,1)S(1)} %bitcast.9), channel_id=1, source_target_pairs={{0,4},{1,5},{2,0},{3,1},{4,6},{5,7},{6,2},{7,3},{8,12},{9,13},{10,... | collective-permute-start | bytes 393224 | tf_op jit(solution)/shard_map/ppermute | solution.py:297
  24.0 1.4 %collective-permute-done.1 = bf16[2,256,128]{2,1,0:T(8,128)(2,1)S(1)} collective-permute-done((bf16[2,256,128]{2,1,0:T(8,128)(2,1)S(1)}, bf16[2,256,128]{2,1,0:T(8,128)(2,1)S(1)}, u32[]{:S(2)}, u32[]{:S(2)}) %collective-permute-start.1) | collective-permute-done | bytes 131104 | tf_op jit(solution)/shard_map/ppermute | solution.py:297
  25.4 2.1 %collective-permute-done.2 = bf16[2,256,128]{2,1,0:T(8,128)(2,1)S(1)} collective-permute-done((bf16[2,256,128]{2,1,0:T(8,128)(2,1)S(1)}, bf16[2,256,128]{2,1,0:T(8,128)(2,1)S(1)}, u32[]{:S(2)}, u32[]{:S(2)}) %collective-permute-start.2) | collective-permute-done | bytes 131104 | tf_op jit(solution)/shard_map/ppermute | solution.py:297
  30.1 1.3 %collective-permute-start.20 = (bf16[2,256,128]{2,1,0:T(8,128)(2,1)S(1)}, bf16[2,256,128]{2,1,0:T(8,128)(2,1)S(1)}, u32[]{:S(2)}, u32[]{:S(2)}) collective-permute-start(bf16[2,256,128]{2,1,0:T(8,128)(2,1)S(1)} %shard_map.60.refs_33_), channel_id=1, source_target_pairs={{16,9},{17,8},{18,11},{19,10},{20,13},{21,12},{22,15},{23,14}} | collective-permute-start | bytes 393224 | tf_op jit(solution)/shard_map/ppermute | solution.py:291
  31.4 1.3 %collective-permute-start.21 = (bf16[2,256,128]{2,1,0:T(8,128)(2,1)S(1)}, bf16[2,256,128]{2,1,0:T(8,128)(2,1)S(1)}, u32[]{:S(2)}, u32[]{:S(2)}) collective-permute-start(bf16[2,256,128]{2,1,0:T(8,128)(2,1)S(1)} %shard_map.60.refs_33_), channel_id=1, source_target_pairs={{16,15},{17,14},{18,13},{19,12},{20,11},{21,10},{22,9},{23,8}} | collective-permute-start | bytes 393224 | tf_op jit(solution)/shard_map/ppermute | solution.py:291
  32.7 1.3 %collective-permute-start.22 = (bf16[2,256,128]{2,1,0:T(8,128)(2,1)S(1)}, bf16[2,256,128]{2,1,0:T(8,128)(2,1)S(1)}, u32[]{:S(2)}, u32[]{:S(2)}) collective-permute-start(bf16[2,256,128]{2,1,0:T(8,128)(2,1)S(1)} %shard_map.60.refs_33_), channel_id=1, source_target_pairs={{16,10},{17,11},{18,14},{19,15},{20,8},{21,9},{22,12},{23,13}} | collective-permute-start | bytes 393224 | tf_op jit(solution)/shard_map/ppermute | solution.py:291
  34.0 23.4 %collective-permute-done.19.refs_0_.refs_8_ = bf16[2,256,128]{2,1,0:T(8,128)(2,1)S(1)} collective-permute-done((bf16[2,256,128]{2,1,0:T(8,128)(2,1)S(1)}, bf16[2,256,128]{2,1,0:T(8,128)(2,1)S(1)}, u32[]{:S(2)}, u32[]{:S(2)}) %collective-permute-start.19) | collective-permute-done | bytes 131104 | tf_op jit(solution)/shard_map/ppermute | solution.py:291
  61.0 1.3 %collective-permute-start.25 = (bf16[2,256,128]{2,1,0:T(8,128)(2,1)S(1)}, bf16[2,256,128]{2,1,0:T(8,128)(2,1)S(1)}, u32[]{:S(2)}, u32[]{:S(2)}) collective-permute-start(bf16[2,256,128]{2,1,0:T(8,128)(2,1)S(1)} %shard_map.60.refs_33_), channel_id=1, source_target_pairs={{16,13},{17,12},{18,9},{19,8},{20,15},{21,14},{22,11},{23,10}} | collective-permute-start | bytes 393224 | tf_op jit(solution)/shard_map/ppermute | solution.py:291
  62.3 1.3 %collective-permute-start.26 = (bf16[2,256,128]{2,1,0:T(8,128)(2,1)S(1)}, bf16[2,256,128]{2,1,0:T(8,128)(2,1)S(1)}, u32[]{:S(2)}, u32[]{:S(2)}) collective-permute-start(bf16[2,256,128]{2,1,0:T(8,128)(2,1)S(1)} %shard_map.60.refs_33_), channel_id=1, source_target_pairs={{16,8},{17,9},{18,10},{19,11},{20,12},{21,13},{22,14},{23,15}} | collective-permute-start | bytes 393224 | tf_op jit(solution)/shard_map/ppermute | solution.py:291
  63.6 4.2 %collective-permute-done.23.refs_4_.refs_12_ = bf16[2,256,128]{2,1,0:T(8,128)(2,1)S(1)} collective-permute-done((bf16[2,256,128]{2,1,0:T(8,128)(2,1)S(1)}, bf16[2,256,128]{2,1,0:T(8,128)(2,1)S(1)}, u32[]{:S(2)}, u32[]{:S(2)}) %collective-permute-start.23) | collective-permute-done | bytes 131104 | tf_op jit(solution)/shard_map/ppermute | solution.py:291
  67.8 1.4 %collective-permute-done.25.refs_6_.refs_14_ = bf16[2,256,128]{2,1,0:T(8,128)(2,1)S(1)} collective-permute-done((bf16[2,256,128]{2,1,0:T(8,128)(2,1)S(1)}, bf16[2,256,128]{2,1,0:T(8,128)(2,1)S(1)}, u32[]{:S(2)}, u32[]{:S(2)}) %collective-permute-start.25) | collective-permute-done | bytes 131104 | tf_op jit(solution)/shard_map/ppermute | solution.py:291
  69.1 1.4 %collective-permute-done.26.refs_7_.refs_15_ = bf16[2,256,128]{2,1,0:T(8,128)(2,1)S(1)} collective-permute-done((bf16[2,256,128]{2,1,0:T(8,128)(2,1)S(1)}, bf16[2,256,128]{2,1,0:T(8,128)(2,1)S(1)}, u32[]{:S(2)}, u32[]{:S(2)}) %collective-permute-start.26) | collective-permute-done | bytes 131104 | tf_op jit(solution)/shard_map/ppermute | solution.py:291
  71.3 1.3 %collective-permute-start.27 = (bf16[2,256,128]{2,1,0:T(8,128)(2,1)S(1)}, bf16[2,256,128]{2,1,0:T(8,128)(2,1)S(1)}, u32[]{:S(2)}, u32[]{:S(2)}) collective-permute-start(bf16[2,256,128]{2,1,0:T(8,128)(2,1)S(1)} %shard_map.62.refs_32_), channel_id=1, source_target_pairs={{8,6},{9,7},{10,4},{11,5},{12,2},{13,3},{14,0},{15,1}} | collective-permute-start | bytes 393224 | tf_op jit(solution)/shard_map/ppermute | solution.py:291
  72.6 1.3 %collective-permute-start.28 = (bf16[2,256,128]{2,1,0:T(8,128)(2,1)S(1)}, bf16[2,256,128]{2,1,0:T(8,128)(2,1)S(1)}, u32[]{:S(2)}, u32[]{:S(2)}) collective-permute-start(bf16[2,256,128]{2,1,0:T(8,128)(2,1)S(1)} %shard_map.62.refs_32_), channel_id=1, source_target_pairs={{8,1},{9,0},{10,3},{11,2},{12,5},{13,4},{14,7},{15,6}} | collective-permute-start | bytes 393224 | tf_op jit(solution)/shard_map/ppermute | solution.py:291
  73.9 1.3 %collective-permute-start.29 = (bf16[2,256,128]{2,1,0:T(8,128)(2,1)S(1)}, bf16[2,256,128]{2,1,0:T(8,128)(2,1)S(1)}, u32[]{:S(2)}, u32[]{:S(2)}) collective-permute-start(bf16[2,256,128]{2,1,0:T(8,128)(2,1)S(1)} %shard_map.62.refs_32_), channel_id=1, source_target_pairs={{8,7},{9,6},{10,5},{11,4},{12,3},{13,2},{14,1},{15,0}} | collective-permute-start | bytes 393224 | tf_op jit(solution)/shard_map/ppermute | solution.py:291
  75.2 1.3 %collective-permute-start.30 = (bf16[2,256,128]{2,1,0:T(8,128)(2,1)S(1)}, bf16[2,256,128]{2,1,0:T(8,128)(2,1)S(1)}, u32[]{:S(2)}, u32[]{:S(2)}) collective-permute-start(bf16[2,256,128]{2,1,0:T(8,128)(2,1)S(1)} %shard_map.62.refs_32_), channel_id=1, source_target_pairs={{8,2},{9,3},{10,6},{11,7},{12,0},{13,1},{14,4},{15,5}} | collective-permute-start | bytes 393224 | tf_op jit(solution)/shard_map/ppermute | solution.py:291
  76.5 5.9 %collective-permute-start.31 = (bf16[2,256,128]{2,1,0:T(8,128)(2,1)S(1)}, bf16[2,256,128]{2,1,0:T(8,128)(2,1)S(1)}, u32[]{:S(2)}, u32[]{:S(2)}) collective-permute-start(bf16[2,256,128]{2,1,0:T(8,128)(2,1)S(1)} %shard_map.62.refs_32_), channel_id=1, source_target_pairs={{8,3},{9,2},{10,7},{11,6},{12,1},{13,0},{14,5},{15,4}} | collective-permute-start | bytes 393224 | tf_op jit(solution)/shard_map/ppermute | solution.py:291
  82.4 1.5 %collective-permute-start.32 = (bf16[2,256,128]{2,1,0:T(8,128)(2,1)S(1)}, bf16[2,256,128]{2,1,0:T(8,128)(2,1)S(1)}, u32[]{:S(2)}, u32[]{:S(2)}) collective-permute-start(bf16[2,256,128]{2,1,0:T(8,128)(2,1)S(1)} %shard_map.62.refs_32_), channel_id=1, source_target_pairs={{8,4},{9,5},{10,0},{11,1},{12,6},{13,7},{14,2},{15,3}} | collective-permute-start | bytes 393224 | tf_op jit(solution)/shard_map/ppermute | solution.py:291
  83.9 1.6 %collective-permute-start.33 = (bf16[2,256,128]{2,1,0:T(8,128)(2,1)S(1)}, bf16[2,256,128]{2,1,0:T(8,128)(2,1)S(1)}, u32[]{:S(2)}, u32[]{:S(2)}) collective-permute-start(bf16[2,256,128]{2,1,0:T(8,128)(2,1)S(1)} %shard_map.62.refs_32_), channel_id=1, source_target_pairs={{8,5},{9,4},{10,1},{11,0},{12,7},{13,6},{14,3},{15,2}} | collective-permute-start | bytes 393224 | tf_op jit(solution)/shard_map/ppermute | solution.py:291
  85.5 1.3 %collective-permute-start.34 = (bf16[2,256,128]{2,1,0:T(8,128)(2,1)S(1)}, bf16[2,256,128]{2,1,0:T(8,128)(2,1)S(1)}, u32[]{:S(2)}, u32[]{:S(2)}) collective-permute-start(bf16[2,256,128]{2,1,0:T(8,128)(2,1)S(1)} %shard_map.62.refs_32_), channel_id=1, source_target_pairs={{8,0},{9,1},{10,2},{11,3},{12,4},{13,5},{14,6},{15,7}} | collective-permute-start | bytes 393224 | tf_op jit(solution)/shard_map/ppermute | solution.py:291
  86.8 3.2 %shard_map.61.factors_ref = bf16[256,4096]{1,0:T(8,128)(2,1)S(1)} custom-call(s32[1,2048]{1,0:T(1,128)S(1)} %get-tuple-element.9.orders_ref, bf16[4,2,256,128]{3,2,1,0:T(8,128)(2,1)S(1)} %pad_maximum_fusion.refs_0_, bf16[4,2,256,128]{3,2,1,0:T(8,128)(2,1)S(1)} %collective-permute-done.18.refs_1_), custom_call_target="tpu_custom_call" | custom-call | tf_op jit(solution)/shard_map/pallas_call | solution.py:64
  90.0 7.6 %shard_map.63 = (f32[1,2,512]{2,1,0:T(2,128)}, bf16[1,2,256,128]{3,2,1,0:T(8,128)(2,1)}) custom-call(bf16[2,256,2048]{2,1,0:T(8,128)(2,1)S(1)} %get-tuple-element.8.matrix_ref, s32[1,2048]{1,0:T(1,128)S(1)} %get-tuple-element.9.orders_ref, bf16[256,4096]{1,0:T(8,128)(2,1)S(1)} %shard_map.61.factors_ref, ...), custom_call_target="tpu_custom_call" | custom-call | tf_op jit(solution)/shard_map/pallas_call | solution.py:64
  (55 shorter events, 19.3 us)
Async XLA Ops:
  0.6 9.7 %collective-permute-start.3 = (bf16[2,256,128]{2,1,0:T(8,128)(2,1)}, bf16[2,256,128]{2,1,0:T(8,128)(2,1)S(1)}, u32[]{:S(2)}, u32[]{:S(2)}) collective-permute-start(bf16[2,256,128]{2,1,0:T(8,128)(2,1)} %refs_1_.1), channel_id=1, source_target_pairs={{8,30},{9,31},{10,28},{11,29},{12,26},{13,27},{14,24},{15,25}} | collective-permute-start | bytes 393224 | tf_op jit(solution)/shard_map/ppermute | solution.py:291
  8.3 5.0 %collective-permute-start.5 = (bf16[2,256,128]{2,1,0:T(8,128)(2,1)}, bf16[2,256,128]{2,1,0:T(8,128)(2,1)S(1)}, u32[]{:S(2)}, u32[]{:S(2)}) collective-permute-start(bf16[2,256,128]{2,1,0:T(8,128)(2,1)} %refs_1_.1), channel_id=1, source_target_pairs={{16,31},{17,30},{18,29},{19,28},{20,27},{21,26},{22,25},{23,24}} | collective-permute-start | bytes 393224 | tf_op jit(solution)/shard_map/ppermute | solution.py:291
  9.0 4.4 %collective-permute-start.6 = (bf16[2,256,128]{2,1,0:T(8,128)(2,1)}, bf16[2,256,128]{2,1,0:T(8,128)(2,1)S(1)}, u32[]{:S(2)}, u32[]{:S(2)}) collective-permute-start(bf16[2,256,128]{2,1,0:T(8,128)(2,1)} %refs_1_.1), channel_id=1, source_target_pairs={{0,26},{1,27},{2,30},{3,31},{4,24},{5,25},{6,28},{7,29}} | collective-permute-start | bytes 393224 | tf_op jit(solution)/shard_map/ppermute | solution.py:291
  18.2 5.8 %collective-permute-start = (bf16[2,256,128]{2,1,0:T(8,128)(2,1)S(1)}, bf16[2,256,128]{2,1,0:T(8,128)(2,1)S(1)}, u32[]{:S(2)}, u32[]{:S(2)}) collective-permute-start(bf16[2,256,128]{2,1,0:T(8,128)(2,1)S(1)} %bitcast.7), channel_id=1, source_target_pairs={{0,6},{1,7},{2,4},{3,5},{4,2},{5,3},{6,0},{7,1},{8,14},{9,15},{10,... | collective-permute-start | bytes 393224 | tf_op jit(solution)/shard_map/ppermute | solution.py:297
  18.3 3.8 %collective-permute-start.16 = (bf16[2,256,128]{2,1,0:T(8,128)(2,1)S(1)}, bf16[2,256,128]{2,1,0:T(8,128)(2,1)S(1)}, u32[]{:S(2)}, u32[]{:S(2)}) collective-permute-start(bf16[2,256,128]{2,1,0:T(8,128)(2,1)S(1)} %shard_map.59.refs_34_), channel_id=1, source_target_pairs={{24,21},{25,20},{26,17},{27,16},{28,23},{29,22},{30,19},{31,18}} | collective-permute-start | bytes 393224 | tf_op jit(solution)/shard_map/ppermute | solution.py:291
  19.7 5.7 %collective-permute-start.1 = (bf16[2,256,128]{2,1,0:T(8,128)(2,1)S(1)}, bf16[2,256,128]{2,1,0:T(8,128)(2,1)S(1)}, u32[]{:S(2)}, u32[]{:S(2)}) collective-permute-start(bf16[2,256,128]{2,1,0:T(8,128)(2,1)S(1)} %bitcast.8), channel_id=1, source_target_pairs={{0,2},{1,3},{2,6},{3,7},{4,0},{5,1},{6,4},{7,5},{8,10},{9,11},{10,... | collective-permute-start | bytes 393224 | tf_op jit(solution)/shard_map/ppermute | solution.py:297
  20.0 7.5 %collective-permute-start.2 = (bf16[2,256,128]{2,1,0:T(8,128)(2,1)S(1)}, bf16[2,256,128]{2,1,0:T(8,128)(2,1)S(1)}, u32[]{:S(2)}, u32[]{:S(2)}) collective-permute-start(bf16[2,256,128]{2,1,0:T(8,128)(2,1)S(1)} %bitcast.9), channel_id=1, source_target_pairs={{0,4},{1,5},{2,0},{3,1},{4,6},{5,7},{6,2},{7,3},{8,12},{9,13},{10,... | collective-permute-start | bytes 393224 | tf_op jit(solution)/shard_map/ppermute | solution.py:297
  27.6 57.9 %collective-permute-start.18 = (bf16[4,2,256,128]{3,2,1,0:T(8,128)(2,1)S(1)}, bf16[4,2,256,128]{3,2,1,0:T(8,128)(2,1)S(1)}, u32[]{:S(2)}, u32[]{:S(2)}) collective-permute-start(bf16[4,2,256,128]{3,2,1,0:T(8,128)(2,1)S(1)} %pad_maximum_fusion.refs_0_), channel_id=1, source_target_pairs={{0,1},{1,0},{2,3},{3,2},{4,5},{5,4},{6,7},{7,6},{8,9},{9,8},{10,11... | collective-permute-start | bytes 1572872 | tf_op jit(solution)/shard_map/ppermute | solution.py:297
  28.8 28.5 %collective-permute-start.19 = (bf16[2,256,128]{2,1,0:T(8,128)(2,1)S(1)}, bf16[2,256,128]{2,1,0:T(8,128)(2,1)S(1)}, u32[]{:S(2)}, u32[]{:S(2)}) collective-permute-start(bf16[2,256,128]{2,1,0:T(8,128)(2,1)S(1)} %shard_map.60.refs_33_), channel_id=1, source_target_pairs={{16,14},{17,15},{18,12},{19,13},{20,10},{21,11},{22,8},{23,9}} | collective-permute-start | bytes 393224 | tf_op jit(solution)/shard_map/ppermute | solution.py:291
  30.1 29.6 %collective-permute-start.20 = (bf16[2,256,128]{2,1,0:T(8,128)(2,1)S(1)}, bf16[2,256,128]{2,1,0:T(8,128)(2,1)S(1)}, u32[]{:S(2)}, u32[]{:S(2)}) collective-permute-start(bf16[2,256,128]{2,1,0:T(8,128)(2,1)S(1)} %shard_map.60.refs_33_), channel_id=1, source_target_pairs={{16,9},{17,8},{18,11},{19,10},{20,13},{21,12},{22,15},{23,14}} | collective-permute-start | bytes 393224 | tf_op jit(solution)/shard_map/ppermute | solution.py:291
  31.4 29.6 %collective-permute-start.21 = (bf16[2,256,128]{2,1,0:T(8,128)(2,1)S(1)}, bf16[2,256,128]{2,1,0:T(8,128)(2,1)S(1)}, u32[]{:S(2)}, u32[]{:S(2)}) collective-permute-start(bf16[2,256,128]{2,1,0:T(8,128)(2,1)S(1)} %shard_map.60.refs_33_), channel_id=1, source_target_pairs={{16,15},{17,14},{18,13},{19,12},{20,11},{21,10},{22,9},{23,8}} | collective-permute-start | bytes 393224 | tf_op jit(solution)/shard_map/ppermute | solution.py:291
  32.7 29.6 %collective-permute-start.22 = (bf16[2,256,128]{2,1,0:T(8,128)(2,1)S(1)}, bf16[2,256,128]{2,1,0:T(8,128)(2,1)S(1)}, u32[]{:S(2)}, u32[]{:S(2)}) collective-permute-start(bf16[2,256,128]{2,1,0:T(8,128)(2,1)S(1)} %shard_map.60.refs_33_), channel_id=1, source_target_pairs={{16,10},{17,11},{18,14},{19,15},{20,8},{21,9},{22,12},{23,13}} | collective-permute-start | bytes 393224 | tf_op jit(solution)/shard_map/ppermute | solution.py:291
  57.3 10.4 %collective-permute-start.23 = (bf16[2,256,128]{2,1,0:T(8,128)(2,1)S(1)}, bf16[2,256,128]{2,1,0:T(8,128)(2,1)S(1)}, u32[]{:S(2)}, u32[]{:S(2)}) collective-permute-start(bf16[2,256,128]{2,1,0:T(8,128)(2,1)S(1)} %shard_map.60.refs_33_), channel_id=1, source_target_pairs={{16,11},{17,10},{18,15},{19,14},{20,9},{21,8},{22,13},{23,12}} | collective-permute-start | bytes 393224 | tf_op jit(solution)/shard_map/ppermute | solution.py:291
  59.7 8.1 %collective-permute-start.24 = (bf16[2,256,128]{2,1,0:T(8,128)(2,1)S(1)}, bf16[2,256,128]{2,1,0:T(8,128)(2,1)S(1)}, u32[]{:S(2)}, u32[]{:S(2)}) collective-permute-start(bf16[2,256,128]{2,1,0:T(8,128)(2,1)S(1)} %shard_map.60.refs_33_), channel_id=1, source_target_pairs={{16,12},{17,13},{18,8},{19,9},{20,14},{21,15},{22,10},{23,11}} | collective-permute-start | bytes 393224 | tf_op jit(solution)/shard_map/ppermute | solution.py:291
  61.0 8.2 %collective-permute-start.25 = (bf16[2,256,128]{2,1,0:T(8,128)(2,1)S(1)}, bf16[2,256,128]{2,1,0:T(8,128)(2,1)S(1)}, u32[]{:S(2)}, u32[]{:S(2)}) collective-permute-start(bf16[2,256,128]{2,1,0:T(8,128)(2,1)S(1)} %shard_map.60.refs_33_), channel_id=1, source_target_pairs={{16,13},{17,12},{18,9},{19,8},{20,15},{21,14},{22,11},{23,10}} | collective-permute-start | bytes 393224 | tf_op jit(solution)/shard_map/ppermute | solution.py:291
  62.3 8.3 %collective-permute-start.26 = (bf16[2,256,128]{2,1,0:T(8,128)(2,1)S(1)}, bf16[2,256,128]{2,1,0:T(8,128)(2,1)S(1)}, u32[]{:S(2)}, u32[]{:S(2)}) collective-permute-start(bf16[2,256,128]{2,1,0:T(8,128)(2,1)S(1)} %shard_map.60.refs_33_), channel_id=1, source_target_pairs={{16,8},{17,9},{18,10},{19,11},{20,12},{21,13},{22,14},{23,15}} | collective-permute-start | bytes 393224 | tf_op jit(solution)/shard_map/ppermute | solution.py:291
  71.3 5.2 %collective-permute-start.27 = (bf16[2,256,128]{2,1,0:T(8,128)(2,1)S(1)}, bf16[2,256,128]{2,1,0:T(8,128)(2,1)S(1)}, u32[]{:S(2)}, u32[]{:S(2)}) collective-permute-start(bf16[2,256,128]{2,1,0:T(8,128)(2,1)S(1)} %shard_map.62.refs_32_), channel_id=1, source_target_pairs={{8,6},{9,7},{10,4},{11,5},{12,2},{13,3},{14,0},{15,1}} | collective-permute-start | bytes 393224 | tf_op jit(solution)/shard_map/ppermute | solution.py:291
  72.6 9.8 %collective-permute-start.28 = (bf16[2,256,128]{2,1,0:T(8,128)(2,1)S(1)}, bf16[2,256,128]{2,1,0:T(8,128)(2,1)S(1)}, u32[]{:S(2)}, u32[]{:S(2)}) collective-permute-start(bf16[2,256,128]{2,1,0:T(8,128)(2,1)S(1)} %shard_map.62.refs_32_), channel_id=1, source_target_pairs={{8,1},{9,0},{10,3},{11,2},{12,5},{13,4},{14,7},{15,6}} | collective-permute-start | bytes 393224 | tf_op jit(solution)/shard_map/ppermute | solution.py:291
  73.9 10.0 %collective-permute-start.29 = (bf16[2,256,128]{2,1,0:T(8,128)(2,1)S(1)}, bf16[2,256,128]{2,1,0:T(8,128)(2,1)S(1)}, u32[]{:S(2)}, u32[]{:S(2)}) collective-permute-start(bf16[2,256,128]{2,1,0:T(8,128)(2,1)S(1)} %shard_map.62.refs_32_), channel_id=1, source_target_pairs={{8,7},{9,6},{10,5},{11,4},{12,3},{13,2},{14,1},{15,0}} | collective-permute-start | bytes 393224 | tf_op jit(solution)/shard_map/ppermute | solution.py:291
  75.2 14.8 %collective-permute-start.30 = (bf16[2,256,128]{2,1,0:T(8,128)(2,1)S(1)}, bf16[2,256,128]{2,1,0:T(8,128)(2,1)S(1)}, u32[]{:S(2)}, u32[]{:S(2)}) collective-permute-start(bf16[2,256,128]{2,1,0:T(8,128)(2,1)S(1)} %shard_map.62.refs_32_), channel_id=1, source_target_pairs={{8,2},{9,3},{10,6},{11,7},{12,0},{13,1},{14,4},{15,5}} | collective-permute-start | bytes 393224 | tf_op jit(solution)/shard_map/ppermute | solution.py:291
  76.5 13.5 %collective-permute-start.31 = (bf16[2,256,128]{2,1,0:T(8,128)(2,1)S(1)}, bf16[2,256,128]{2,1,0:T(8,128)(2,1)S(1)}, u32[]{:S(2)}, u32[]{:S(2)}) collective-permute-start(bf16[2,256,128]{2,1,0:T(8,128)(2,1)S(1)} %shard_map.62.refs_32_), channel_id=1, source_target_pairs={{8,3},{9,2},{10,7},{11,6},{12,1},{13,0},{14,5},{15,4}} | collective-permute-start | bytes 393224 | tf_op jit(solution)/shard_map/ppermute | solution.py:291
  82.4 7.6 %collective-permute-start.32 = (bf16[2,256,128]{2,1,0:T(8,128)(2,1)S(1)}, bf16[2,256,128]{2,1,0:T(8,128)(2,1)S(1)}, u32[]{:S(2)}, u32[]{:S(2)}) collective-permute-start(bf16[2,256,128]{2,1,0:T(8,128)(2,1)S(1)} %shard_map.62.refs_32_), channel_id=1, source_target_pairs={{8,4},{9,5},{10,0},{11,1},{12,6},{13,7},{14,2},{15,3}} | collective-permute-start | bytes 393224 | tf_op jit(solution)/shard_map/ppermute | solution.py:291
  83.9 6.1 %collective-permute-start.33 = (bf16[2,256,128]{2,1,0:T(8,128)(2,1)S(1)}, bf16[2,256,128]{2,1,0:T(8,128)(2,1)S(1)}, u32[]{:S(2)}, u32[]{:S(2)}) collective-permute-start(bf16[2,256,128]{2,1,0:T(8,128)(2,1)S(1)} %shard_map.62.refs_32_), channel_id=1, source_target_pairs={{8,5},{9,4},{10,1},{11,0},{12,7},{13,6},{14,3},{15,2}} | collective-permute-start | bytes 393224 | tf_op jit(solution)/shard_map/ppermute | solution.py:291
  85.5 4.5 %collective-permute-start.34 = (bf16[2,256,128]{2,1,0:T(8,128)(2,1)S(1)}, bf16[2,256,128]{2,1,0:T(8,128)(2,1)S(1)}, u32[]{:S(2)}, u32[]{:S(2)}) collective-permute-start(bf16[2,256,128]{2,1,0:T(8,128)(2,1)S(1)} %shard_map.62.refs_32_), channel_id=1, source_target_pairs={{8,0},{9,1},{10,2},{11,3},{12,4},{13,5},{14,6},{15,7}} | collective-permute-start | bytes 393224 | tf_op jit(solution)/shard_map/ppermute | solution.py:291
  (12 other events, 38.3 us)

commit v2 on v1

--- a/solution.py
+++ b/solution.py
@@ -20,6 +20,7 @@
     "own": (0, 1, 2, 3),
 }
 ORDER = ("far0", "own1", "far1", "out0", "out1", "in0", "in1", "own0")
+EARLY, LATE = list(ORDER[:4]), list(ORDER[4:])
 TURNS = ("far", "out", "in")
 WHOLE = "all"
 
@@ -71,16 +72,24 @@
     )(*[pltpu.with_memory_space_constraint(a, VMEM) for a in args])
 
 
-def product(matrix_ref, pieces):
-    rows = matrix_ref.shape[1]
-    part = jnp.zeros((rows, 2 * LANES), F32)
-    by_re, by_im = part, part
+def partial_product(matrix_ref, pieces, sums):
+    by_re, by_im = sums
     for slot, value in pieces.items():
         size = value.shape[1]
         cols = pl.ds(place(slot, size), size)
         both = jnp.concatenate([value[0], value[1]], axis=1)
         by_re += jnp.dot(matrix_ref[0, :, cols], both, preferred_element_type=F32)
         by_im += jnp.dot(matrix_ref[1, :, cols], both, preferred_element_type=F32)
+    return by_re, by_im
+
+
+def zeros(matrix_ref):
+    part = jnp.zeros((matrix_ref.shape[1], 2 * LANES), F32)
+    return part, part
+
+
+def complex_product(sums):
+    by_re, by_im = sums
     re = by_re[:, :LANES] - by_im[:, LANES:]
     im = by_re[:, LANES:] + by_im[:, :LANES]
     return re.astype(BF16), im.astype(BF16)
@@ -91,7 +100,8 @@
 
     def body(matrix_ref, *refs):
         out_ref = refs[-1]
-        re, im = product(matrix_ref, {slot: read(refs, e) for slot, e in spots.items()})
+        pieces = {slot: read(refs, e) for slot, e in spots.items()}
+        re, im = complex_product(partial_product(matrix_ref, pieces, zeros(matrix_ref)))
         out_ref[0] = re
         out_ref[1] = im
 
@@ -173,47 +183,105 @@
     )
 
 
-def finish(matrix, orders, factors, sets, belows, band, scale):
+def chosen_pieces(refs, maps, slots):
+    layer = lax.axis_index("layer")
+    last = {slot: read(refs, maps[0][slot]) for slot in slots}
+    own = dict(last)
+    for index in range(1, len(maps)):
+        for slot in slots:
+            own[slot] = jnp.where(layer == index, read(refs, maps[index][slot]), own[slot])
+    return last, own
+
+
+def sort_chunks(orders_ref, whole, pieces, rows, band):
+    harmonics = orders_ref.shape[1]
+    first = harmonics - 1 - band * lax.axis_index("harm")
+    held = []
+    spot = 0
+    for slot, value in pieces.items():
+        size = value.shape[1]
+        whole[spot : spot + size, :LANES] = value[0]
+        whole[spot : spot + size, LANES:] = value[1]
+        held.append(orders_ref[:, pl.ds(place(slot, size), size)])
+        spot += size
+    targets = jnp.concatenate(held, axis=1) + first
+    chunk = 5 * LANES if rows % (5 * LANES) == 0 else LANES
+    for row in range(0, rows, chunk):
+        picked = jnp.dot(
+            one_hot(targets, row, chunk), whole[...], preferred_element_type=F32
+        ).astype(BF16)
+        for b in range(chunk // LANES):
+            yield row // LANES + b, picked[b * LANES : (b + 1) * LANES]
+
+
+def begin(matrix, orders, sets, slots, band):
+    rows = matrix.shape[1]
+    harmonics = orders.shape[1]
+    width = 2 * LANES
+    window = harmonics + pl.cdiv(band, LANES) * LANES
+    sets = [{slot: group[slot] for slot in slots} for group in sets]
+    arrays, maps = listed(*sets)
+
+    def body(matrix_ref, orders_ref, *refs):
+        sums_ref, moved_ref, whole = refs[len(arrays) :]
+        last, own = chosen_pieces(refs, maps, slots)
+        by_re, by_im = partial_product(matrix_ref, last, zeros(matrix_ref))
+        sums_ref[0] = by_re
+        sums_ref[1] = by_im
+        for block, picked in sort_chunks(orders_ref, whole, own, window, band):
+            moved_ref[:, block * width : (block + 1) * width] = picked
+
+    return call(
+        body,
+        [VMEM((2, rows, width), F32), VMEM((LANES, window // LANES * width), BF16)],
+        [matrix, orders, *arrays],
+        16,
+        [VMEM((harmonics // len(ORDER) * len(slots), width), BF16)],
+    )
+
+
+def finish(matrix, orders, factors, sets, slots, begun, belows, band, scale):
     layers = len(sets)
     harmonics = orders.shape[1]
     rows = matrix.shape[1]
     blocks = harmonics // LANES
-    bands = band // LANES
-    strip = bands + 1
+    strip = pl.cdiv(band, LANES) + 1
+    width = 2 * LANES
+    sets = [{slot: group[slot] for slot in slots} for group in sets]
     arrays, maps = listed(*sets)
+    window = harmonics + (strip - 1) * LANES
+    held = harmonics if slots == [WHOLE] else harmonics // len(ORDER) * len(slots)
 
     def body(matrix_ref, orders_ref, factors_ref, *refs):
         set_refs, refs = refs[: len(arrays)], refs[len(arrays) :]
         below_refs, refs = refs[: layers - 1], refs[layers - 1 :]
+        begun_refs, refs = refs[: len(begun)], refs[len(begun) :]
         grad_ref, bottom_ref, whole, moved = refs
         layer = lax.axis_index("layer")
-        last = {slot: read(set_refs, e) for slot, e in maps[0].items()}
-        chosen = dict(last)
-        for index in range(1, layers):
-            for slot, entry in maps[index].items():
-                chosen[slot] = jnp.where(layer == index, read(set_refs, entry), chosen[slot])
-        fill(whole, chosen)
-        re, im = product(matrix_ref, last)
+        last, own = chosen_pieces(set_refs, maps, slots)
+        sums = (begun_refs[0][0], begun_refs[0][1]) if begun else zeros(matrix_ref)
+        re, im = complex_product(partial_product(matrix_ref, last, sums))
         for index in range(1, layers):
             re = jnp.where(layer == index, below_refs[index - 1][0], re)
             im = jnp.where(layer == index, below_refs[index - 1][1], im)
         bottom_ref[0, 0] = re
         bottom_ref[0, 1] = im
 
-        targets = orders_ref[...] + (harmonics - 1 - band * lax.axis_index("harm"))
-        for c in range(blocks + bands):
-            picked = jnp.dot(
-                one_hot(targets, c * LANES, LANES), whole[...], preferred_element_type=F32
-            ).astype(BF16)
-            moved[:, c * 2 * LANES : (c + 1) * 2 * LANES] = picked
-        width = 2 * LANES
+        for block, picked in sort_chunks(orders_ref, whole, own, window, band):
+            here = slice(block * width, (block + 1) * width)
+            if begun:
+                picked += begun_refs[1][:, here]
+            moved[:LANES, here] = picked
+            if block > 0:
+                moved[LANES:, (block - 1) * width : block * width] = picked
         length = blocks * width
         parts = []
-        for q in range(strip):
+        for q in range(0, strip, 2):
+            height = width if q + 1 < strip else LANES
             parts.append(
                 lax.dot_general(
                     factors_ref[...],
-                    moved[:, q * width : q * width + length],
+                    moved[:height, q * width : q * width + length],
                     (((1,), (1,)), ((), ())),
                     preferred_element_type=F32,
                 )
@@ -238,11 +306,11 @@
     return call(
         body,
         outs,
-        [matrix, orders, factors, *arrays, *belows],
+        [matrix, orders, factors, *arrays, *belows, *begun],
         24,
         [
-            VMEM((harmonics, 2 * LANES), BF16),
-            VMEM((LANES, (blocks + bands) * 2 * LANES), BF16),
+            VMEM((held, width), BF16),
+            VMEM((2 * LANES, (blocks + strip - 1) * width), BF16),
         ],
     )
 
@@ -277,7 +345,9 @@
         sets.append(group)
         belows.append(below)
     factors = sort_fields(table, gathered(fields[0]))
-    return finish(matrix, table, factors, sets[::-1], belows[::-1], band, scale)
+    return finish(
+        matrix, table, factors, sets[::-1], [WHOLE], [], belows[::-1], band, scale
+    )
 
 
 def direct_sweep(source, transfer, fields, orders):
@@ -320,11 +390,14 @@
         held[turn + "0"] = (mine, part)
         held[turn + "1"] = (beside, part)
     factors = sort_fields(table, held)
-    return finish(matrix, table, factors, sets[::-1], belows[::-1], band, scale)
+    begun = begin(matrix, table, sets[::-1], EARLY, band)
+    return finish(
+        matrix, table, factors, sets[::-1], LATE, begun, belows[::-1], band, scale
+    )
 
 
 def solution(mesh):
-    return jax.shard_map(
+    step = jax.shard_map(
         sweep,
         mesh=mesh,
         in_specs=(
@@ -336,3 +409,6 @@
         out_specs=(P("layer", None, "harm"), P("layer", None, "harm", None)),
         check_vma=False,
     )
+    if mesh.shape["harm"] != len(ORDER):
+        return step
+    return step

time: 98.2 us -> 94 us (0.957)
  the two profiles are of different devices: /device:TPU:1 before, /device:TPU:0 now
where the time goes in v2:
time: 94 us; the launch traced here: 93.4 us
  starting transfers between devices  41.6 us (44%)
  waiting for transfers between devices  37.4 us (40%)
  Pallas kernels  13.2 us (14%)
  between operations  1.13 us (1%)
    ppermute x31, starting transfers between devices, move(): return lax.ppermute(value, ('layer', 'harm'), pairs)  35.9 us
    ppermute x31, waiting for transfers between devices, move(): return lax.ppermute(value, ('layer', 'harm'), pairs)  33.9 us
    pallas_call x6, Pallas kernels, call(): pl.pallas_call(body, out_shape=outs, in_specs=[spec] * len(args), out_spe...  11.6 us
    ppermute x4, starting transfers between devices, among(): return lax.ppermute(value, ('layer', 'harm'), pairs)  5.65 us
    ppermute x4, waiting for transfers between devices, among(): return lax.ppermute(value, ('layer', 'harm'), pairs)  3.49 us
  transfers between devices with their start and end apart: 35, of which 7 were waited for; matrix products, arithmetic and copies ran while one was open for 0% of the time, Pallas kernels for 9%

profile of v2, /device:TPU:0, one launch (start us, length us, event | category | flops | bytes accessed | tf_op | source)
XLA Modules:
  0.0 93.4 jit_solution(15798096427036075085)
XLA Ops:
  1.3 6.0 %collective-permute-start.6 = (bf16[2,256,128]{2,1,0:T(8,128)(2,1)}, bf16[2,256,128]{2,1,0:T(8,128)(2,1)S(1)}, u32[]{:S(2)}, u32[]{:S(2)}) collective-permute-start(bf16[2,256,128]{2,1,0:T(8,128)(2,1)} %refs_1_.1), channel_id=1, source_target_pairs={{0,26},{1,27},{2,30},{3,31},{4,24},{5,25},{6,28},{7,29}} | collective-permute-start | bytes 393224 | tf_op jit(solution)/shard_map/ppermute | solution.py:361
  7.9 1.9 %collective-permute-start.4 = (bf16[2,256,128]{2,1,0:T(8,128)(2,1)}, bf16[2,256,128]{2,1,0:T(8,128)(2,1)S(1)}, u32[]{:S(2)}, u32[]{:S(2)}) collective-permute-start(bf16[2,256,128]{2,1,0:T(8,128)(2,1)} %refs_1_.1), channel_id=1, source_target_pairs={{0,25},{1,24},{2,27},{3,26},{4,29},{5,28},{6,31},{7,30}} | collective-permute-start | bytes 393224 | tf_op jit(solution)/shard_map/ppermute | solution.py:361
  11.2 4.5 %collective-permute-start.8 = (bf16[2,256,128]{2,1,0:T(8,128)(2,1)}, bf16[2,256,128]{2,1,0:T(8,128)(2,1)S(1)}, u32[]{:S(2)}, u32[]{:S(2)}) collective-permute-start(bf16[2,256,128]{2,1,0:T(8,128)(2,1)} %refs_1_.1), channel_id=1, source_target_pairs={{0,28},{1,29},{2,24},{3,25},{4,30},{5,31},{6,26},{7,27}} | collective-permute-start | bytes 393224 | tf_op jit(solution)/shard_map/ppermute | solution.py:361
  15.7 1.6 %bring.1 = (bf16[2,256,2048]{2,1,0:T(8,128)(2,1)S(1)}, bf16[2,256,128]{2,1,0:T(8,128)(2,1)S(1)}, s32[1,2048]{1,0:T(1,128)S(1)}) custom-call(bf16[2,256,2048]{2,1,0:T(8,128)(2,1)} %bitcast.6, bf16[2,256,128]{2,1,0:T(8,128)(2,1)} %refs_1_.1, s32[1,2048]{1,0:T(1,128)} %bitcast.13), custom_call_target="tpu_custom_call" | custom-call | tf_op jit(solution)/shard_map/bring/pallas_call | solution.py:139
  17.4 1.1 %collective-permute-done.8.refs_6_.refs_13_ = bf16[2,256,128]{2,1,0:T(8,128)(2,1)S(1)} collective-permute-done((bf16[2,256,128]{2,1,0:T(8,128)(2,1)}, bf16[2,256,128]{2,1,0:T(8,128)(2,1)S(1)}, u32[]{:S(2)}, u32[]{:S(2)}) %collective-permute-start.8) | collective-permute-done | bytes 131104 | tf_op jit(solution)/shard_map/ppermute | solution.py:361
  24.7 2.5 %collective-permute-start.2 = (bf16[2,256,128]{2,1,0:T(8,128)(2,1)S(1)}, bf16[2,256,128]{2,1,0:T(8,128)(2,1)S(1)}, u32[]{:S(2)}, u32[]{:S(2)}) collective-permute-start(bf16[2,256,128]{2,1,0:T(8,128)(2,1)S(1)} %bitcast.7), channel_id=1, source_target_pairs={{0,4},{1,5},{2,0},{3,1},{4,6},{5,7},{6,2},{7,3},{8,12},{9,13},{10,... | collective-permute-start | bytes 393224 | tf_op jit(solution)/shard_map/ppermute | solution.py:367
  27.2 1.5 %collective-permute-start = (bf16[2,256,128]{2,1,0:T(8,128)(2,1)S(1)}, bf16[2,256,128]{2,1,0:T(8,128)(2,1)S(1)}, u32[]{:S(2)}, u32[]{:S(2)}) collective-permute-start(bf16[2,256,128]{2,1,0:T(8,128)(2,1)S(1)} %bitcast.9), channel_id=1, source_target_pairs={{0,6},{1,7},{2,4},{3,5},{4,2},{5,3},{6,0},{7,1},{8,14},{9,15},{10,... | collective-permute-start | bytes 393224 | tf_op jit(solution)/shard_map/ppermute | solution.py:367
  31.8 3.2 %collective-permute-done.1 = bf16[2,256,128]{2,1,0:T(8,128)(2,1)S(1)} collective-permute-done((bf16[2,256,128]{2,1,0:T(8,128)(2,1)S(1)}, bf16[2,256,128]{2,1,0:T(8,128)(2,1)S(1)}, u32[]{:S(2)}, u32[]{:S(2)}) %collective-permute-start.1) | collective-permute-done | bytes 131104 | tf_op jit(solution)/shard_map/ppermute | solution.py:367
  35.7 1.6 %collective-permute-start.18 = (bf16[4,2,256,128]{3,2,1,0:T(8,128)(2,1)S(1)}, bf16[4,2,256,128]{3,2,1,0:T(8,128)(2,1)S(1)}, u32[]{:S(2)}, u32[]{:S(2)}) collective-permute-start(bf16[4,2,256,128]{3,2,1,0:T(8,128)(2,1)S(1)} %pad_maximum_fusion.refs_0_), channel_id=1, source_target_pairs={{0,1},{1,0},{2,3},{3,2},{4,5},{5,4},{6,7},{7,6},{8,9},{9,8},{10,11... | collective-permute-start | bytes 1572872 | tf_op jit(solution)/shard_map/ppermute | solution.py:367
  40.8 1.3 %collective-permute-start.34 = (bf16[2,256,128]{2,1,0:T(8,128)(2,1)S(1)}, bf16[2,256,128]{2,1,0:T(8,128)(2,1)S(1)}, u32[]{:S(2)}, u32[]{:S(2)}) collective-permute-start(bf16[2,256,128]{2,1,0:T(8,128)(2,1)S(1)} %shard_map.62.refs_16_), channel_id=1, source_target_pairs={{8,2},{9,3},{10,6},{11,7},{12,0},{13,1},{14,4},{15,5}} | collective-permute-start | bytes 393224 | tf_op jit(solution)/shard_map/ppermute | solution.py:361
  42.1 1.3 %collective-permute-start.33 = (bf16[2,256,128]{2,1,0:T(8,128)(2,1)S(1)}, bf16[2,256,128]{2,1,0:T(8,128)(2,1)S(1)}, u32[]{:S(2)}, u32[]{:S(2)}) collective-permute-start(bf16[2,256,128]{2,1,0:T(8,128)(2,1)S(1)} %shard_map.62.refs_16_), channel_id=1, source_target_pairs={{8,7},{9,6},{10,5},{11,4},{12,3},{13,2},{14,1},{15,0}} | collective-permute-start | bytes 393224 | tf_op jit(solution)/shard_map/ppermute | solution.py:361
  43.4 1.3 %collective-permute-start.32 = (bf16[2,256,128]{2,1,0:T(8,128)(2,1)S(1)}, bf16[2,256,128]{2,1,0:T(8,128)(2,1)S(1)}, u32[]{:S(2)}, u32[]{:S(2)}) collective-permute-start(bf16[2,256,128]{2,1,0:T(8,128)(2,1)S(1)} %shard_map.62.refs_16_), channel_id=1, source_target_pairs={{8,1},{9,0},{10,3},{11,2},{12,5},{13,4},{14,7},{15,6}} | collective-permute-start | bytes 393224 | tf_op jit(solution)/shard_map/ppermute | solution.py:361
  44.7 1.3 %collective-permute-start.31 = (bf16[2,256,128]{2,1,0:T(8,128)(2,1)S(1)}, bf16[2,256,128]{2,1,0:T(8,128)(2,1)S(1)}, u32[]{:S(2)}, u32[]{:S(2)}) collective-permute-start(bf16[2,256,128]{2,1,0:T(8,128)(2,1)S(1)} %shard_map.62.refs_16_), channel_id=1, source_target_pairs={{8,6},{9,7},{10,4},{11,5},{12,2},{13,3},{14,0},{15,1}} | collective-permute-start | bytes 393224 | tf_op jit(solution)/shard_map/ppermute | solution.py:361
  46.0 25.4 %collective-permute-done.34.refs_3_ = bf16[2,256,128]{2,1,0:T(8,128)(2,1)S(1)} collective-permute-done((bf16[2,256,128]{2,1,0:T(8,128)(2,1)S(1)}, bf16[2,256,128]{2,1,0:T(8,128)(2,1)S(1)}, u32[]{:S(2)}, u32[]{:S(2)}) %collective-permute-start.34) | collective-permute-done | bytes 131104 | tf_op jit(solution)/shard_map/ppermute | solution.py:361
  71.4 1.3 %collective-permute-start.30 = (bf16[2,256,128]{2,1,0:T(8,128)(2,1)S(1)}, bf16[2,256,128]{2,1,0:T(8,128)(2,1)S(1)}, u32[]{:S(2)}, u32[]{:S(2)}) collective-permute-start(bf16[2,256,128]{2,1,0:T(8,128)(2,1)S(1)} %shard_map.62.refs_16_), channel_id=1, source_target_pairs={{8,0},{9,1},{10,2},{11,3},{12,4},{13,5},{14,6},{15,7}} | collective-permute-start | bytes 393224 | tf_op jit(solution)/shard_map/ppermute | solution.py:361
  72.7 3.7 %collective-permute-done.33.refs_2_ = bf16[2,256,128]{2,1,0:T(8,128)(2,1)S(1)} collective-permute-done((bf16[2,256,128]{2,1,0:T(8,128)(2,1)S(1)}, bf16[2,256,128]{2,1,0:T(8,128)(2,1)S(1)}, u32[]{:S(2)}, u32[]{:S(2)}) %collective-permute-start.33) | collective-permute-done | bytes 131104 | tf_op jit(solution)/shard_map/ppermute | solution.py:361
  76.4 1.3 %collective-permute-start.29 = (bf16[2,256,128]{2,1,0:T(8,128)(2,1)S(1)}, bf16[2,256,128]{2,1,0:T(8,128)(2,1)S(1)}, u32[]{:S(2)}, u32[]{:S(2)}) collective-permute-start(bf16[2,256,128]{2,1,0:T(8,128)(2,1)S(1)} %shard_map.62.refs_16_), channel_id=1, source_target_pairs={{8,5},{9,4},{10,1},{11,0},{12,7},{13,6},{14,3},{15,2}} | collective-permute-start | bytes 393224 | tf_op jit(solution)/shard_map/ppermute | solution.py:361
  77.7 1.0 %collective-permute-done.32.refs_1_ = bf16[2,256,128]{2,1,0:T(8,128)(2,1)S(1)} collective-permute-done((bf16[2,256,128]{2,1,0:T(8,128)(2,1)S(1)}, bf16[2,256,128]{2,1,0:T(8,128)(2,1)S(1)}, u32[]{:S(2)}, u32[]{:S(2)}) %collective-permute-start.32) | collective-permute-done | bytes 131104 | tf_op jit(solution)/shard_map/ppermute | solution.py:361
  78.6 1.3 %collective-permute-start.28 = (bf16[2,256,128]{2,1,0:T(8,128)(2,1)S(1)}, bf16[2,256,128]{2,1,0:T(8,128)(2,1)S(1)}, u32[]{:S(2)}, u32[]{:S(2)}) collective-permute-start(bf16[2,256,128]{2,1,0:T(8,128)(2,1)S(1)} %shard_map.62.refs_16_), channel_id=1, source_target_pairs={{8,4},{9,5},{10,0},{11,1},{12,6},{13,7},{14,2},{15,3}} | collective-permute-start | bytes 393224 | tf_op jit(solution)/shard_map/ppermute | solution.py:361
  80.0 1.3 %collective-permute-start.27 = (bf16[2,256,128]{2,1,0:T(8,128)(2,1)S(1)}, bf16[2,256,128]{2,1,0:T(8,128)(2,1)S(1)}, u32[]{:S(2)}, u32[]{:S(2)}) collective-permute-start(bf16[2,256,128]{2,1,0:T(8,128)(2,1)S(1)} %shard_map.62.refs_16_), channel_id=1, source_target_pairs={{8,3},{9,2},{10,7},{11,6},{12,1},{13,0},{14,5},{15,4}} | collective-permute-start | bytes 393224 | tf_op jit(solution)/shard_map/ppermute | solution.py:361
  81.2 1.9 %shard_map.63 = (f32[2,256,256]{2,1,0:T(8,128)S(1)}, bf16[128,5120]{1,0:T(8,128)(2,1)S(1)}) custom-call(bf16[2,256,2048]{2,1,0:T(8,128)(2,1)S(1)} %get-tuple-element.10.matrix_ref, s32[1,2048]{1,0:T(1,128)S(1)} %get-tuple-element.11.orders_ref, bf16[2,256,128]{2,1,0:T(8,128)(2,1)S(1)} %collective-permute-done.31.refs_0_, ...), custom_call_target="tpu_custom_call" | custom-call | tf_op jit(solution)/shard_map/pallas_call | solution.py:65
  83.2 3.2 %shard_map.61.factors_ref = bf16[256,4096]{1,0:T(8,128)(2,1)S(1)} custom-call(s32[1,2048]{1,0:T(1,128)S(1)} %get-tuple-element.11.orders_ref, bf16[4,2,256,128]{3,2,1,0:T(8,128)(2,1)S(1)} %pad_maximum_fusion.refs_0_, bf16[4,2,256,128]{3,2,1,0:T(8,128)(2,1)S(1)} %collective-permute-done.18.refs_1_), custom_call_target="tpu_custom_call" | custom-call | tf_op jit(solution)/shard_map/pallas_call | solution.py:65
  86.4 2.7 %collective-permute-done.27.refs_0_ = bf16[2,256,128]{2,1,0:T(8,128)(2,1)S(1)} collective-permute-done((bf16[2,256,128]{2,1,0:T(8,128)(2,1)S(1)}, bf16[2,256,128]{2,1,0:T(8,128)(2,1)S(1)}, u32[]{:S(2)}, u32[]{:S(2)}) %collective-permute-start.27) | collective-permute-done | bytes 131104 | tf_op jit(solution)/shard_map/ppermute | solution.py:361
  89.0 4.4 %shard_map.64 = (f32[1,2,512]{2,1,0:T(2,128)}, bf16[1,2,256,128]{3,2,1,0:T(8,128)(2,1)}) custom-call(bf16[2,256,2048]{2,1,0:T(8,128)(2,1)S(1)} %get-tuple-element.10.matrix_ref, s32[1,2048]{1,0:T(1,128)S(1)} %get-tuple-element.11.orders_ref, bf16[256,4096]{1,0:T(8,128)(2,1)S(1)} %shard_map.61.factors_ref, ...), custom_call_target="tpu_custom_call" | custom-call | tf_op jit(solution)/shard_map/pallas_call | solution.py:65
  (56 shorter events, 15.9 us)
Async XLA Ops:
  0.6 9.9 %collective-permute-start.7 = (bf16[2,256,128]{2,1,0:T(8,128)(2,1)}, bf16[2,256,128]{2,1,0:T(8,128)(2,1)S(1)}, u32[]{:S(2)}, u32[]{:S(2)}) collective-permute-start(bf16[2,256,128]{2,1,0:T(8,128)(2,1)} %refs_1_.1), channel_id=1, source_target_pairs={{16,27},{17,26},{18,31},{19,30},{20,25},{21,24},{22,29},{23,28}} | collective-permute-start | bytes 393224 | tf_op jit(solution)/shard_map/ppermute | solution.py:361
  1.3 9.9 %collective-permute-start.6 = (bf16[2,256,128]{2,1,0:T(8,128)(2,1)}, bf16[2,256,128]{2,1,0:T(8,128)(2,1)S(1)}, u32[]{:S(2)}, u32[]{:S(2)}) collective-permute-start(bf16[2,256,128]{2,1,0:T(8,128)(2,1)} %refs_1_.1), channel_id=1, source_target_pairs={{0,26},{1,27},{2,30},{3,31},{4,24},{5,25},{6,28},{7,29}} | collective-permute-start | bytes 393224 | tf_op jit(solution)/shard_map/ppermute | solution.py:361
  7.3 10.1 %collective-permute-start.5 = (bf16[2,256,128]{2,1,0:T(8,128)(2,1)}, bf16[2,256,128]{2,1,0:T(8,128)(2,1)S(1)}, u32[]{:S(2)}, u32[]{:S(2)}) collective-permute-start(bf16[2,256,128]{2,1,0:T(8,128)(2,1)} %refs_1_.1), channel_id=1, source_target_pairs={{16,31},{17,30},{18,29},{19,28},{20,27},{21,26},{22,25},{23,24}} | collective-permute-start | bytes 393224 | tf_op jit(solution)/shard_map/ppermute | solution.py:361
  7.9 9.4 %collective-permute-start.4 = (bf16[2,256,128]{2,1,0:T(8,128)(2,1)}, bf16[2,256,128]{2,1,0:T(8,128)(2,1)S(1)}, u32[]{:S(2)}, u32[]{:S(2)}) collective-permute-start(bf16[2,256,128]{2,1,0:T(8,128)(2,1)} %refs_1_.1), channel_id=1, source_target_pairs={{0,25},{1,24},{2,27},{3,26},{4,29},{5,28},{6,31},{7,30}} | collective-permute-start | bytes 393224 | tf_op jit(solution)/shard_map/ppermute | solution.py:361
  9.8 7.5 %collective-permute-start.3 = (bf16[2,256,128]{2,1,0:T(8,128)(2,1)}, bf16[2,256,128]{2,1,0:T(8,128)(2,1)S(1)}, u32[]{:S(2)}, u32[]{:S(2)}) collective-permute-start(bf16[2,256,128]{2,1,0:T(8,128)(2,1)} %refs_1_.1), channel_id=1, source_target_pairs={{8,30},{9,31},{10,28},{11,29},{12,26},{13,27},{14,24},{15,25}} | collective-permute-start | bytes 393224 | tf_op jit(solution)/shard_map/ppermute | solution.py:361
  10.5 6.9 %collective-permute-start.9 = (bf16[2,256,128]{2,1,0:T(8,128)(2,1)}, bf16[2,256,128]{2,1,0:T(8,128)(2,1)S(1)}, u32[]{:S(2)}, u32[]{:S(2)}) collective-permute-start(bf16[2,256,128]{2,1,0:T(8,128)(2,1)} %refs_1_.1), channel_id=1, source_target_pairs={{16,29},{17,28},{18,25},{19,24},{20,31},{21,30},{22,27},{23,26}} | collective-permute-start | bytes 393224 | tf_op jit(solution)/shard_map/ppermute | solution.py:361
  11.2 7.3 %collective-permute-start.8 = (bf16[2,256,128]{2,1,0:T(8,128)(2,1)}, bf16[2,256,128]{2,1,0:T(8,128)(2,1)S(1)}, u32[]{:S(2)}, u32[]{:S(2)}) collective-permute-start(bf16[2,256,128]{2,1,0:T(8,128)(2,1)} %refs_1_.1), channel_id=1, source_target_pairs={{0,28},{1,29},{2,24},{3,25},{4,30},{5,31},{6,26},{7,27}} | collective-permute-start | bytes 393224 | tf_op jit(solution)/shard_map/ppermute | solution.py:361
  21.9 5.3 %collective-permute-start.13 = (bf16[2,256,128]{2,1,0:T(8,128)(2,1)S(1)}, bf16[2,256,128]{2,1,0:T(8,128)(2,1)S(1)}, u32[]{:S(2)}, u32[]{:S(2)}) collective-permute-start(bf16[2,256,128]{2,1,0:T(8,128)(2,1)S(1)} %shard_map.59.refs_18_), channel_id=1, source_target_pairs={{24,18},{25,19},{26,22},{27,23},{28,16},{29,17},{30,20},{31,21}} | collective-permute-start | bytes 393224 | tf_op jit(solution)/shard_map/ppermute | solution.py:361
  23.3 5.5 %collective-permute-start.11 = (bf16[2,256,128]{2,1,0:T(8,128)(2,1)S(1)}, bf16[2,256,128]{2,1,0:T(8,128)(2,1)S(1)}, u32[]{:S(2)}, u32[]{:S(2)}) collective-permute-start(bf16[2,256,128]{2,1,0:T(8,128)(2,1)S(1)} %shard_map.59.refs_18_), channel_id=1, source_target_pairs={{24,17},{25,16},{26,19},{27,18},{28,21},{29,20},{30,23},{31,22}} | collective-permute-start | bytes 393224 | tf_op jit(solution)/shard_map/ppermute | solution.py:361
  24.7 6.4 %collective-permute-start.2 = (bf16[2,256,128]{2,1,0:T(8,128)(2,1)S(1)}, bf16[2,256,128]{2,1,0:T(8,128)(2,1)S(1)}, u32[]{:S(2)}, u32[]{:S(2)}) collective-permute-start(bf16[2,256,128]{2,1,0:T(8,128)(2,1)S(1)} %bitcast.7), channel_id=1, source_target_pairs={{0,4},{1,5},{2,0},{3,1},{4,6},{5,7},{6,2},{7,3},{8,12},{9,13},{10,... | collective-permute-start | bytes 393224 | tf_op jit(solution)/shard_map/ppermute | solution.py:367
  27.2 7.8 %collective-permute-start.1 = (bf16[2,256,128]{2,1,0:T(8,128)(2,1)S(1)}, bf16[2,256,128]{2,1,0:T(8,128)(2,1)S(1)}, u32[]{:S(2)}, u32[]{:S(2)}) collective-permute-start(bf16[2,256,128]{2,1,0:T(8,128)(2,1)S(1)} %bitcast.8), channel_id=1, source_target_pairs={{0,2},{1,3},{2,6},{3,7},{4,0},{5,1},{6,4},{7,5},{8,10},{9,11},{10,... | collective-permute-start | bytes 393224 | tf_op jit(solution)/shard_map/ppermute | solution.py:367
  27.2 8.4 %collective-permute-start = (bf16[2,256,128]{2,1,0:T(8,128)(2,1)S(1)}, bf16[2,256,128]{2,1,0:T(8,128)(2,1)S(1)}, u32[]{:S(2)}, u32[]{:S(2)}) collective-permute-start(bf16[2,256,128]{2,1,0:T(8,128)(2,1)S(1)} %bitcast.9), channel_id=1, source_target_pairs={{0,6},{1,7},{2,4},{3,5},{4,2},{5,3},{6,0},{7,1},{8,14},{9,15},{10,... | collective-permute-start | bytes 393224 | tf_op jit(solution)/shard_map/ppermute | solution.py:367
  29.5 7.8 %collective-permute-start.26 = (bf16[2,256,128]{2,1,0:T(8,128)(2,1)S(1)}, bf16[2,256,128]{2,1,0:T(8,128)(2,1)S(1)}, u32[]{:S(2)}, u32[]{:S(2)}) collective-permute-start(bf16[2,256,128]{2,1,0:T(8,128)(2,1)S(1)} %shard_map.60.refs_17_), channel_id=1, source_target_pairs={{16,8},{17,9},{18,10},{19,11},{20,12},{21,13},{22,14},{23,15}} | collective-permute-start | bytes 393224 | tf_op jit(solution)/shard_map/ppermute | solution.py:361
  30.1 7.8 %collective-permute-start.25 = (bf16[2,256,128]{2,1,0:T(8,128)(2,1)S(1)}, bf16[2,256,128]{2,1,0:T(8,128)(2,1)S(1)}, u32[]{:S(2)}, u32[]{:S(2)}) collective-permute-start(bf16[2,256,128]{2,1,0:T(8,128)(2,1)S(1)} %shard_map.60.refs_17_), channel_id=1, source_target_pairs={{16,13},{17,12},{18,9},{19,8},{20,15},{21,14},{22,11},{23,10}} | collective-permute-start | bytes 393224 | tf_op jit(solution)/shard_map/ppermute | solution.py:361
  31.1 7.6 %collective-permute-start.24 = (bf16[2,256,128]{2,1,0:T(8,128)(2,1)S(1)}, bf16[2,256,128]{2,1,0:T(8,128)(2,1)S(1)}, u32[]{:S(2)}, u32[]{:S(2)}) collective-permute-start(bf16[2,256,128]{2,1,0:T(8,128)(2,1)S(1)} %shard_map.60.refs_17_), channel_id=1, source_target_pairs={{16,12},{17,13},{18,8},{19,9},{20,14},{21,15},{22,10},{23,11}} | collective-permute-start | bytes 393224 | tf_op jit(solution)/shard_map/ppermute | solution.py:361
  35.7 47.4 %collective-permute-start.18 = (bf16[4,2,256,128]{3,2,1,0:T(8,128)(2,1)S(1)}, bf16[4,2,256,128]{3,2,1,0:T(8,128)(2,1)S(1)}, u32[]{:S(2)}, u32[]{:S(2)}) collective-permute-start(bf16[4,2,256,128]{3,2,1,0:T(8,128)(2,1)S(1)} %pad_maximum_fusion.refs_0_), channel_id=1, source_target_pairs={{0,1},{1,0},{2,3},{3,2},{4,5},{5,4},{6,7},{7,6},{8,9},{9,8},{10,11... | collective-permute-start | bytes 1572872 | tf_op jit(solution)/shard_map/ppermute | solution.py:367
  40.8 30.6 %collective-permute-start.34 = (bf16[2,256,128]{2,1,0:T(8,128)(2,1)S(1)}, bf16[2,256,128]{2,1,0:T(8,128)(2,1)S(1)}, u32[]{:S(2)}, u32[]{:S(2)}) collective-permute-start(bf16[2,256,128]{2,1,0:T(8,128)(2,1)S(1)} %shard_map.62.refs_16_), channel_id=1, source_target_pairs={{8,2},{9,3},{10,6},{11,7},{12,0},{13,1},{14,4},{15,5}} | collective-permute-start | bytes 393224 | tf_op jit(solution)/shard_map/ppermute | solution.py:361
  42.1 34.3 %collective-permute-start.33 = (bf16[2,256,128]{2,1,0:T(8,128)(2,1)S(1)}, bf16[2,256,128]{2,1,0:T(8,128)(2,1)S(1)}, u32[]{:S(2)}, u32[]{:S(2)}) collective-permute-start(bf16[2,256,128]{2,1,0:T(8,128)(2,1)S(1)} %shard_map.62.refs_16_), channel_id=1, source_target_pairs={{8,7},{9,6},{10,5},{11,4},{12,3},{13,2},{14,1},{15,0}} | collective-permute-start | bytes 393224 | tf_op jit(solution)/shard_map/ppermute | solution.py:361
  43.4 35.2 %collective-permute-start.32 = (bf16[2,256,128]{2,1,0:T(8,128)(2,1)S(1)}, bf16[2,256,128]{2,1,0:T(8,128)(2,1)S(1)}, u32[]{:S(2)}, u32[]{:S(2)}) collective-permute-start(bf16[2,256,128]{2,1,0:T(8,128)(2,1)S(1)} %shard_map.62.refs_16_), channel_id=1, source_target_pairs={{8,1},{9,0},{10,3},{11,2},{12,5},{13,4},{14,7},{15,6}} | collective-permute-start | bytes 393224 | tf_op jit(solution)/shard_map/ppermute | solution.py:361
  44.7 35.3 %collective-permute-start.31 = (bf16[2,256,128]{2,1,0:T(8,128)(2,1)S(1)}, bf16[2,256,128]{2,1,0:T(8,128)(2,1)S(1)}, u32[]{:S(2)}, u32[]{:S(2)}) collective-permute-start(bf16[2,256,128]{2,1,0:T(8,128)(2,1)S(1)} %shard_map.62.refs_16_), channel_id=1, source_target_pairs={{8,6},{9,7},{10,4},{11,5},{12,2},{13,3},{14,0},{15,1}} | collective-permute-start | bytes 393224 | tf_op jit(solution)/shard_map/ppermute | solution.py:361
  71.4 15.0 %collective-permute-start.30 = (bf16[2,256,128]{2,1,0:T(8,128)(2,1)S(1)}, bf16[2,256,128]{2,1,0:T(8,128)(2,1)S(1)}, u32[]{:S(2)}, u32[]{:S(2)}) collective-permute-start(bf16[2,256,128]{2,1,0:T(8,128)(2,1)S(1)} %shard_map.62.refs_16_), channel_id=1, source_target_pairs={{8,0},{9,1},{10,2},{11,3},{12,4},{13,5},{14,6},{15,7}} | collective-permute-start | bytes 393224 | tf_op jit(solution)/shard_map/ppermute | solution.py:361
  76.4 10.0 %collective-permute-start.29 = (bf16[2,256,128]{2,1,0:T(8,128)(2,1)S(1)}, bf16[2,256,128]{2,1,0:T(8,128)(2,1)S(1)}, u32[]{:S(2)}, u32[]{:S(2)}) collective-permute-start(bf16[2,256,128]{2,1,0:T(8,128)(2,1)S(1)} %shard_map.62.refs_16_), channel_id=1, source_target_pairs={{8,5},{9,4},{10,1},{11,0},{12,7},{13,6},{14,3},{15,2}} | collective-permute-start | bytes 393224 | tf_op jit(solution)/shard_map/ppermute | solution.py:361
  78.6 7.7 %collective-permute-start.28 = (bf16[2,256,128]{2,1,0:T(8,128)(2,1)S(1)}, bf16[2,256,128]{2,1,0:T(8,128)(2,1)S(1)}, u32[]{:S(2)}, u32[]{:S(2)}) collective-permute-start(bf16[2,256,128]{2,1,0:T(8,128)(2,1)S(1)} %shard_map.62.refs_16_), channel_id=1, source_target_pairs={{8,4},{9,5},{10,0},{11,1},{12,6},{13,7},{14,2},{15,3}} | collective-permute-start | bytes 393224 | tf_op jit(solution)/shard_map/ppermute | solution.py:361
  80.0 9.1 %collective-permute-start.27 = (bf16[2,256,128]{2,1,0:T(8,128)(2,1)S(1)}, bf16[2,256,128]{2,1,0:T(8,128)(2,1)S(1)}, u32[]{:S(2)}, u32[]{:S(2)}) collective-permute-start(bf16[2,256,128]{2,1,0:T(8,128)(2,1)S(1)} %shard_map.62.refs_16_), channel_id=1, source_target_pairs={{8,3},{9,2},{10,7},{11,6},{12,1},{13,0},{14,5},{15,4}} | collective-permute-start | bytes 393224 | tf_op jit(solution)/shard_map/ppermute | solution.py:361
  (12 other events, 41.6 us)

commit v3 on v2

--- a/solution.py
+++ b/solution.py
@@ -17,11 +17,14 @@
     "far": (3, 2, 1, 0),
     "out": (1, 3, 0, 2),
     "in": (2, 0, 3, 1),
+    "near": (1, 0, 3, 2),
+    "skip": (2, 3, 0, 1),
     "own": (0, 1, 2, 3),
 }
 ORDER = ("far0", "own1", "far1", "out0", "out1", "in0", "in1", "own0")
 EARLY, LATE = list(ORDER[:4]), list(ORDER[4:])
-TURNS = ("far", "out", "in")
+SENT = [slot for slot in ORDER if slot != "own0"]
+QUAD = ("near", "far", "own", "skip")
 WHOLE = "all"
 
 
@@ -121,9 +124,7 @@
         whole[rows, LANES:] = value[1]
 
 
-def bring(matrix, source, orders):
-    args = [matrix, source, orders]
-
+def bring(*args):
     def body(*refs):
         size = len(args)
         ins, outs, sems = refs[:size], refs[size : 2 * size], refs[-1]
@@ -335,7 +336,7 @@
     def gathered(value):
         return {WHOLE: (lax.all_gather(value, "harm", axis=1, tiled=True), None)}
 
-    matrix, _, table = bring(transfer[0], source, orders.reshape(1, -1))
+    matrix, table = bring(transfer[0], orders.reshape(1, -1))
     group = gathered(source)
     sets, belows = [group], []
     for layer in range(layers - 1, 0, -1):
@@ -366,12 +367,13 @@
         ]
         return lax.ppermute(value, ("layer", "harm"), pairs)
 
-    matrix, own, table = bring(transfer[0], source, orders.reshape(1, -1))
+    matrix, own = bring(transfer[0], source)
+    (table,) = bring(orders.reshape(1, -1))
     group = {"own0": (own, None)}
-    for slot in ORDER[:-1]:
+    for slot in SENT:
         origin = top - 1 if slot[-1] == "1" and slot != "own1" else len(group) % split
         group[slot] = (move(source, origin, top, slot), None)
-    along = [among(fields[0], range(layers), turn + "0") for turn in TURNS]
+    skipped = among(fields[0], range(layers), "skip0")
 
     sets, belows = [group], []
     for layer in range(top, 0, -1):
@@ -381,12 +383,16 @@
             group[slot] = (move(below, layer, layer - 1, slot), None)
         sets.append(group)
         belows.append(below)
+        if layer == top:
+            skipped, _ = lax.optimization_barrier((skipped, below))
+            pair = jnp.stack([fields[0], skipped])
+            near = among(pair, range(layers), "near0")
         if layer == top - 1:
-            along, _ = lax.optimization_barrier((along, below))
-            mine = jnp.stack([*along, fields[0]])
+            near, _ = lax.optimization_barrier((near, below))
+            mine = jnp.concatenate([near, pair])
             beside = among(mine, range(layers), "own1")
     held = {}
-    for part, turn in enumerate((*TURNS, "own")):
+    for part, turn in enumerate(QUAD):
         held[turn + "0"] = (mine, part)
         held[turn + "1"] = (beside, part)
     factors = sort_fields(table, held)

time: 94 us -> 92.3 us (0.982)
  the two profiles are of different devices: /device:TPU:0 before, /device:TPU:1 now
where the time goes in v3:
time: 92.3 us; the launch traced here: 91.7 us
  starting transfers between devices  47.3 us (51%)
  waiting for transfers between devices  29.2 us (32%)
  Pallas kernels  13.9 us (15%)
  between operations  1.18 us (1%)
    ppermute x31, starting transfers between devices, move(): return lax.ppermute(value, ('layer', 'harm'), pairs)  45.9 us
    ppermute x31, waiting for transfers between devices, move(): return lax.ppermute(value, ('layer', 'harm'), pairs)  24.6 us
    pallas_call x6, Pallas kernels, call(): pl.pallas_call(body, out_shape=outs, in_specs=[spec] * len(args), out_spe...  11.6 us
    ppermute x3, waiting for transfers between devices, among(): return lax.ppermute(value, ('layer', 'harm'), pairs)  4.62 us
    pallas_call x2, Pallas kernels, bring(): pl.pallas_call(body, out_shape=[VMEM(a.shape, a.dtype) for a in args], in...  2.32 us
  transfers between devices with their start and end apart: 34, of which 8 were waited for; matrix products, arithmetic and copies ran while one was open for 0% of the time, Pallas kernels for 10%

profile of v3, /device:TPU:1, one launch (start us, length us, event | category | flops | bytes accessed | tf_op | source)
XLA Modules:
  0.0 91.7 jit_solution(12769313316288519823)
XLA Ops:
  3.3 9.5 %collective-permute-start.1 = (bf16[2,256,128]{2,1,0:T(8,128)(2,1)}, bf16[2,256,128]{2,1,0:T(8,128)(2,1)S(1)}, u32[]{:S(2)}, u32[]{:S(2)}) collective-permute-start(bf16[2,256,128]{2,1,0:T(8,128)(2,1)} %refs_1_.1), channel_id=1, source_target_pairs={{8,30},{9,31},{10,28},{11,29},{12,26},{13,27},{14,24},{15,25}} | collective-permute-start | bytes 393224 | tf_op jit(solution)/shard_map/ppermute | solution.py:362
  14.3 1.6 %bring.2 = (bf16[2,256,2048]{2,1,0:T(8,128)(2,1)S(1)}, bf16[2,256,128]{2,1,0:T(8,128)(2,1)S(1)}) custom-call(bf16[2,256,2048]{2,1,0:T(8,128)(2,1)} %bitcast.4, bf16[2,256,128]{2,1,0:T(8,128)(2,1)} %refs_1_.1), custom_call_target="tpu_custom_call" | custom-call | tf_op jit(solution)/shard_map/bring/pallas_call | solution.py:140
  19.4 4.6 %collective-permute-done = bf16[2,256,128]{2,1,0:T(8,128)(2,1)S(1)} collective-permute-done((bf16[2,256,128]{2,1,0:T(8,128)(2,1)}, bf16[2,256,128]{2,1,0:T(8,128)(2,1)S(1)}, u32[]{:S(2)}, u32[]{:S(2)}) %collective-permute-start) | collective-permute-done | bytes 131104 | tf_op jit(solution)/shard_map/ppermute | solution.py:368
  27.6 1.3 %collective-permute-start.25 = (bf16[2,256,128]{2,1,0:T(8,128)(2,1)S(1)}, bf16[2,256,128]{2,1,0:T(8,128)(2,1)S(1)}, u32[]{:S(2)}, u32[]{:S(2)}) collective-permute-start(bf16[2,256,128]{2,1,0:T(8,128)(2,1)S(1)} %shard_map.60.refs_17_), channel_id=1, source_target_pairs={{16,8},{17,9},{18,10},{19,11},{20,12},{21,13},{22,14},{23,15}} | collective-permute-start | bytes 393224 | tf_op jit(solution)/shard_map/ppermute | solution.py:362
  28.9 1.3 %collective-permute-start.24 = (bf16[2,256,128]{2,1,0:T(8,128)(2,1)S(1)}, bf16[2,256,128]{2,1,0:T(8,128)(2,1)S(1)}, u32[]{:S(2)}, u32[]{:S(2)}) collective-permute-start(bf16[2,256,128]{2,1,0:T(8,128)(2,1)S(1)} %shard_map.60.refs_17_), channel_id=1, source_target_pairs={{16,13},{17,12},{18,9},{19,8},{20,15},{21,14},{22,11},{23,10}} | collective-permute-start | bytes 393224 | tf_op jit(solution)/shard_map/ppermute | solution.py:362
  30.2 1.3 %collective-permute-start.23 = (bf16[2,256,128]{2,1,0:T(8,128)(2,1)S(1)}, bf16[2,256,128]{2,1,0:T(8,128)(2,1)S(1)}, u32[]{:S(2)}, u32[]{:S(2)}) collective-permute-start(bf16[2,256,128]{2,1,0:T(8,128)(2,1)S(1)} %shard_map.60.refs_17_), channel_id=1, source_target_pairs={{16,12},{17,13},{18,8},{19,9},{20,14},{21,15},{22,10},{23,11}} | collective-permute-start | bytes 393224 | tf_op jit(solution)/shard_map/ppermute | solution.py:362
  31.5 1.3 %collective-permute-start.22 = (bf16[2,256,128]{2,1,0:T(8,128)(2,1)S(1)}, bf16[2,256,128]{2,1,0:T(8,128)(2,1)S(1)}, u32[]{:S(2)}, u32[]{:S(2)}) collective-permute-start(bf16[2,256,128]{2,1,0:T(8,128)(2,1)S(1)} %shard_map.60.refs_17_), channel_id=1, source_target_pairs={{16,11},{17,10},{18,15},{19,14},{20,9},{21,8},{22,13},{23,12}} | collective-permute-start | bytes 393224 | tf_op jit(solution)/shard_map/ppermute | solution.py:362
  32.9 1.3 %collective-permute-start.17 = (bf16[4,2,256,128]{3,2,1,0:T(8,128)(2,1)S(1)}, bf16[4,2,256,128]{3,2,1,0:T(8,128)(2,1)S(1)}, u32[]{:S(2)}, u32[]{:S(2)}) collective-permute-start(bf16[4,2,256,128]{3,2,1,0:T(8,128)(2,1)S(1)} %pad_maximum_fusion.refs_0_), channel_id=1, source_target_pairs={{0,1},{1,0},{2,3},{3,2},{4,5},{5,4},{6,7},{7,6},{8,9},{9,8},{10,11... | collective-permute-start | bytes 1572872 | tf_op jit(solution)/shard_map/ppermute | solution.py:368
  34.2 13.9 %collective-permute-done.25.refs_7_ = bf16[2,256,128]{2,1,0:T(8,128)(2,1)S(1)} collective-permute-done((bf16[2,256,128]{2,1,0:T(8,128)(2,1)S(1)}, bf16[2,256,128]{2,1,0:T(8,128)(2,1)S(1)}, u32[]{:S(2)}, u32[]{:S(2)}) %collective-permute-start.25) | collective-permute-done | bytes 131104 | tf_op jit(solution)/shard_map/ppermute | solution.py:362
  49.4 1.9 %collective-permute-done.24.refs_6_ = bf16[2,256,128]{2,1,0:T(8,128)(2,1)S(1)} collective-permute-done((bf16[2,256,128]{2,1,0:T(8,128)(2,1)S(1)}, bf16[2,256,128]{2,1,0:T(8,128)(2,1)S(1)}, u32[]{:S(2)}, u32[]{:S(2)}) %collective-permute-start.24) | collective-permute-done | bytes 131104 | tf_op jit(solution)/shard_map/ppermute | solution.py:362
  54.8 1.3 %collective-permute-start.18 = (bf16[2,256,128]{2,1,0:T(8,128)(2,1)S(1)}, bf16[2,256,128]{2,1,0:T(8,128)(2,1)S(1)}, u32[]{:S(2)}, u32[]{:S(2)}) collective-permute-start(bf16[2,256,128]{2,1,0:T(8,128)(2,1)S(1)} %shard_map.60.refs_17_), channel_id=1, source_target_pairs={{16,14},{17,15},{18,12},{19,13},{20,10},{21,11},{22,8},{23,9}} | collective-permute-start | bytes 393224 | tf_op jit(solution)/shard_map/ppermute | solution.py:362
  56.2 5.0 %collective-permute-done.20.refs_2_.refs_6_ = bf16[2,256,128]{2,1,0:T(8,128)(2,1)S(1)} collective-permute-done((bf16[2,256,128]{2,1,0:T(8,128)(2,1)S(1)}, bf16[2,256,128]{2,1,0:T(8,128)(2,1)S(1)}, u32[]{:S(2)}, u32[]{:S(2)}) %collective-permute-start.20) | collective-permute-done | bytes 131104 | tf_op jit(solution)/shard_map/ppermute | solution.py:362
  61.2 1.8 %collective-permute-done.19.refs_1_.refs_5_ = bf16[2,256,128]{2,1,0:T(8,128)(2,1)S(1)} collective-permute-done((bf16[2,256,128]{2,1,0:T(8,128)(2,1)S(1)}, bf16[2,256,128]{2,1,0:T(8,128)(2,1)S(1)}, u32[]{:S(2)}, u32[]{:S(2)}) %collective-permute-start.19) | collective-permute-done | bytes 131104 | tf_op jit(solution)/shard_map/ppermute | solution.py:362
  64.6 1.3 %collective-permute-start.33 = (bf16[2,256,128]{2,1,0:T(8,128)(2,1)S(1)}, bf16[2,256,128]{2,1,0:T(8,128)(2,1)S(1)}, u32[]{:S(2)}, u32[]{:S(2)}) collective-permute-start(bf16[2,256,128]{2,1,0:T(8,128)(2,1)S(1)} %shard_map.62.refs_16_), channel_id=1, source_target_pairs={{8,2},{9,3},{10,6},{11,7},{12,0},{13,1},{14,4},{15,5}} | collective-permute-start | bytes 393224 | tf_op jit(solution)/shard_map/ppermute | solution.py:362
  65.9 1.3 %collective-permute-start.32 = (bf16[2,256,128]{2,1,0:T(8,128)(2,1)S(1)}, bf16[2,256,128]{2,1,0:T(8,128)(2,1)S(1)}, u32[]{:S(2)}, u32[]{:S(2)}) collective-permute-start(bf16[2,256,128]{2,1,0:T(8,128)(2,1)S(1)} %shard_map.62.refs_16_), channel_id=1, source_target_pairs={{8,7},{9,6},{10,5},{11,4},{12,3},{13,2},{14,1},{15,0}} | collective-permute-start | bytes 393224 | tf_op jit(solution)/shard_map/ppermute | solution.py:362
  67.2 1.3 %collective-permute-start.31 = (bf16[2,256,128]{2,1,0:T(8,128)(2,1)S(1)}, bf16[2,256,128]{2,1,0:T(8,128)(2,1)S(1)}, u32[]{:S(2)}, u32[]{:S(2)}) collective-permute-start(bf16[2,256,128]{2,1,0:T(8,128)(2,1)S(1)} %shard_map.62.refs_16_), channel_id=1, source_target_pairs={{8,1},{9,0},{10,3},{11,2},{12,5},{13,4},{14,7},{15,6}} | collective-permute-start | bytes 393224 | tf_op jit(solution)/shard_map/ppermute | solution.py:362
  68.5 1.3 %collective-permute-start.30 = (bf16[2,256,128]{2,1,0:T(8,128)(2,1)S(1)}, bf16[2,256,128]{2,1,0:T(8,128)(2,1)S(1)}, u32[]{:S(2)}, u32[]{:S(2)}) collective-permute-start(bf16[2,256,128]{2,1,0:T(8,128)(2,1)S(1)} %shard_map.62.refs_16_), channel_id=1, source_target_pairs={{8,6},{9,7},{10,4},{11,5},{12,2},{13,3},{14,0},{15,1}} | collective-permute-start | bytes 393224 | tf_op jit(solution)/shard_map/ppermute | solution.py:362
  69.8 4.2 %collective-permute-start.29 = (bf16[2,256,128]{2,1,0:T(8,128)(2,1)S(1)}, bf16[2,256,128]{2,1,0:T(8,128)(2,1)S(1)}, u32[]{:S(2)}, u32[]{:S(2)}) collective-permute-start(bf16[2,256,128]{2,1,0:T(8,128)(2,1)S(1)} %shard_map.62.refs_16_), channel_id=1, source_target_pairs={{8,0},{9,1},{10,2},{11,3},{12,4},{13,5},{14,6},{15,7}} | collective-permute-start | bytes 393224 | tf_op jit(solution)/shard_map/ppermute | solution.py:362
  74.1 4.7 %collective-permute-start.28 = (bf16[2,256,128]{2,1,0:T(8,128)(2,1)S(1)}, bf16[2,256,128]{2,1,0:T(8,128)(2,1)S(1)}, u32[]{:S(2)}, u32[]{:S(2)}) collective-permute-start(bf16[2,256,128]{2,1,0:T(8,128)(2,1)S(1)} %shard_map.62.refs_16_), channel_id=1, source_target_pairs={{8,5},{9,4},{10,1},{11,0},{12,7},{13,6},{14,3},{15,2}} | collective-permute-start | bytes 393224 | tf_op jit(solution)/shard_map/ppermute | solution.py:362
  78.8 1.3 %collective-permute-start.27 = (bf16[2,256,128]{2,1,0:T(8,128)(2,1)S(1)}, bf16[2,256,128]{2,1,0:T(8,128)(2,1)S(1)}, u32[]{:S(2)}, u32[]{:S(2)}) collective-permute-start(bf16[2,256,128]{2,1,0:T(8,128)(2,1)S(1)} %shard_map.62.refs_16_), channel_id=1, source_target_pairs={{8,4},{9,5},{10,0},{11,1},{12,6},{13,7},{14,2},{15,3}} | collective-permute-start | bytes 393224 | tf_op jit(solution)/shard_map/ppermute | solution.py:362
  80.1 1.3 %collective-permute-start.26 = (bf16[2,256,128]{2,1,0:T(8,128)(2,1)S(1)}, bf16[2,256,128]{2,1,0:T(8,128)(2,1)S(1)}, u32[]{:S(2)}, u32[]{:S(2)}) collective-permute-start(bf16[2,256,128]{2,1,0:T(8,128)(2,1)S(1)} %shard_map.62.refs_16_), channel_id=1, source_target_pairs={{8,3},{9,2},{10,7},{11,6},{12,1},{13,0},{14,5},{15,4}} | collective-permute-start | bytes 393224 | tf_op jit(solution)/shard_map/ppermute | solution.py:362
  82.2 1.9 %shard_map.63 = (f32[2,256,256]{2,1,0:T(8,128)S(1)}, bf16[128,5120]{1,0:T(8,128)(2,1)S(1)}) custom-call(bf16[2,256,2048]{2,1,0:T(8,128)(2,1)S(1)} %get-tuple-element.8.matrix_ref, s32[1,2048]{1,0:T(1,128)S(1)} %bring.3.orders_ref, bf16[2,256,128]{2,1,0:T(8,128)(2,1)S(1)} %collective-permute-done.30.refs_0_, ...), custom_call_target="tpu_custom_call" | custom-call | tf_op jit(solution)/shard_map/pallas_call | solution.py:68
  84.1 3.2 %shard_map.61.factors_ref = bf16[256,4096]{1,0:T(8,128)(2,1)S(1)} custom-call(s32[1,2048]{1,0:T(1,128)S(1)} %bring.3.orders_ref, bf16[4,2,256,128]{3,2,1,0:T(8,128)(2,1)S(1)} %pad_maximum_fusion.refs_0_, bf16[4,2,256,128]{3,2,1,0:T(8,128)(2,1)S(1)} %collective-permute-done.17.refs_1_), custom_call_target="tpu_custom_call" | custom-call | tf_op jit(solution)/shard_map/pallas_call | solution.py:68
  87.3 4.4 %shard_map.64 = (f32[1,2,512]{2,1,0:T(2,128)}, bf16[1,2,256,128]{3,2,1,0:T(8,128)(2,1)}) custom-call(bf16[2,256,2048]{2,1,0:T(8,128)(2,1)S(1)} %get-tuple-element.8.matrix_ref, s32[1,2048]{1,0:T(1,128)S(1)} %bring.3.orders_ref, bf16[256,4096]{1,0:T(8,128)(2,1)S(1)} %shard_map.61.factors_ref, bf16[2,256,128]{2,1,0:T(8,128)(2,1)S(1)} %collective-permute-done.26.refs_0_, ...), custom_call_target="tpu_custom_call" | custom-call | tf_op jit(solution)/shard_map/pallas_call | solution.py:68
  (56 shorter events, 18.3 us)
Async XLA Ops:
  0.6 12.2 %collective-permute-start.5 = (bf16[2,256,128]{2,1,0:T(8,128)(2,1)}, bf16[2,256,128]{2,1,0:T(8,128)(2,1)S(1)}, u32[]{:S(2)}, u32[]{:S(2)}) collective-permute-start(bf16[2,256,128]{2,1,0:T(8,128)(2,1)} %refs_1_.1), channel_id=1, source_target_pairs={{16,27},{17,26},{18,31},{19,30},{20,25},{21,24},{22,29},{23,28}} | collective-permute-start | bytes 393224 | tf_op jit(solution)/shard_map/ppermute | solution.py:362
  1.3 12.2 %collective-permute-start.4 = (bf16[2,256,128]{2,1,0:T(8,128)(2,1)}, bf16[2,256,128]{2,1,0:T(8,128)(2,1)S(1)}, u32[]{:S(2)}, u32[]{:S(2)}) collective-permute-start(bf16[2,256,128]{2,1,0:T(8,128)(2,1)} %refs_1_.1), channel_id=1, source_target_pairs={{0,26},{1,27},{2,30},{3,31},{4,24},{5,25},{6,28},{7,29}} | collective-permute-start | bytes 393224 | tf_op jit(solution)/shard_map/ppermute | solution.py:362
  2.0 12.2 %collective-permute-start.3 = (bf16[2,256,128]{2,1,0:T(8,128)(2,1)}, bf16[2,256,128]{2,1,0:T(8,128)(2,1)S(1)}, u32[]{:S(2)}, u32[]{:S(2)}) collective-permute-start(bf16[2,256,128]{2,1,0:T(8,128)(2,1)} %refs_1_.1), channel_id=1, source_target_pairs={{16,31},{17,30},{18,29},{19,28},{20,27},{21,26},{22,25},{23,24}} | collective-permute-start | bytes 393224 | tf_op jit(solution)/shard_map/ppermute | solution.py:362
  2.7 13.3 %collective-permute-start.2 = (bf16[2,256,128]{2,1,0:T(8,128)(2,1)}, bf16[2,256,128]{2,1,0:T(8,128)(2,1)S(1)}, u32[]{:S(2)}, u32[]{:S(2)}) collective-permute-start(bf16[2,256,128]{2,1,0:T(8,128)(2,1)} %refs_1_.1), channel_id=1, source_target_pairs={{0,25},{1,24},{2,27},{3,26},{4,29},{5,28},{6,31},{7,30}} | collective-permute-start | bytes 393224 | tf_op jit(solution)/shard_map/ppermute | solution.py:362
  3.3 12.6 %collective-permute-start.1 = (bf16[2,256,128]{2,1,0:T(8,128)(2,1)}, bf16[2,256,128]{2,1,0:T(8,128)(2,1)S(1)}, u32[]{:S(2)}, u32[]{:S(2)}) collective-permute-start(bf16[2,256,128]{2,1,0:T(8,128)(2,1)} %refs_1_.1), channel_id=1, source_target_pairs={{8,30},{9,31},{10,28},{11,29},{12,26},{13,27},{14,24},{15,25}} | collective-permute-start | bytes 393224 | tf_op jit(solution)/shard_map/ppermute | solution.py:362
  14.2 9.8 %collective-permute-start = (bf16[2,256,128]{2,1,0:T(8,128)(2,1)}, bf16[2,256,128]{2,1,0:T(8,128)(2,1)S(1)}, u32[]{:S(2)}, u32[]{:S(2)}) collective-permute-start(bf16[2,256,128]{2,1,0:T(8,128)(2,1)} %bitcast.5), channel_id=1, source_target_pairs={{0,4},{1,5},{2,6},{3,7},{4,0},{5,1},{6,2},{7,3},{8,12},{9,13},{10,... | collective-permute-start | bytes 393224 | tf_op jit(solution)/shard_map/ppermute | solution.py:368
  18.0 7.5 %collective-permute-start.14 = (bf16[2,256,128]{2,1,0:T(8,128)(2,1)S(1)}, bf16[2,256,128]{2,1,0:T(8,128)(2,1)S(1)}, u32[]{:S(2)}, u32[]{:S(2)}) collective-permute-start(bf16[2,256,128]{2,1,0:T(8,128)(2,1)S(1)} %shard_map.59.refs_18_), channel_id=1, source_target_pairs={{24,20},{25,21},{26,16},{27,17},{28,22},{29,23},{30,18},{31,19}} | collective-permute-start | bytes 393224 | tf_op jit(solution)/shard_map/ppermute | solution.py:362
  18.7 7.5 %collective-permute-start.13 = (bf16[2,256,128]{2,1,0:T(8,128)(2,1)S(1)}, bf16[2,256,128]{2,1,0:T(8,128)(2,1)S(1)}, u32[]{:S(2)}, u32[]{:S(2)}) collective-permute-start(bf16[2,256,128]{2,1,0:T(8,128)(2,1)S(1)} %shard_map.59.refs_18_), channel_id=1, source_target_pairs={{24,19},{25,18},{26,23},{27,22},{28,17},{29,16},{30,21},{31,20}} | collective-permute-start | bytes 393224 | tf_op jit(solution)/shard_map/ppermute | solution.py:362
  24.0 8.8 %collective-permute-start.8 = (bf16[2,2,256,128]{3,2,1,0:T(8,128)(2,1)S(1)}, bf16[2,2,256,128]{3,2,1,0:T(8,128)(2,1)S(1)}, u32[]{:S(2)}, u32[]{:S(2)}) collective-permute-start(bf16[2,2,256,128]{3,2,1,0:T(8,128)(2,1)S(1)} %pad_maximum_fusion.1), channel_id=1, source_target_pairs={{0,2},{1,3},{2,0},{3,1},{4,6},{5,7},{6,4},{7,5},{8,10},{9,11},{10,... | collective-permute-start | bytes 786440 | tf_op jit(solution)/shard_map/ppermute | solution.py:368
  27.6 20.5 %collective-permute-start.25 = (bf16[2,256,128]{2,1,0:T(8,128)(2,1)S(1)}, bf16[2,256,128]{2,1,0:T(8,128)(2,1)S(1)}, u32[]{:S(2)}, u32[]{:S(2)}) collective-permute-start(bf16[2,256,128]{2,1,0:T(8,128)(2,1)S(1)} %shard_map.60.refs_17_), channel_id=1, source_target_pairs={{16,8},{17,9},{18,10},{19,11},{20,12},{21,13},{22,14},{23,15}} | collective-permute-start | bytes 393224 | tf_op jit(solution)/shard_map/ppermute | solution.py:362
  28.9 22.3 %collective-permute-start.24 = (bf16[2,256,128]{2,1,0:T(8,128)(2,1)S(1)}, bf16[2,256,128]{2,1,0:T(8,128)(2,1)S(1)}, u32[]{:S(2)}, u32[]{:S(2)}) collective-permute-start(bf16[2,256,128]{2,1,0:T(8,128)(2,1)S(1)} %shard_map.60.refs_17_), channel_id=1, source_target_pairs={{16,13},{17,12},{18,9},{19,8},{20,15},{21,14},{22,11},{23,10}} | collective-permute-start | bytes 393224 | tf_op jit(solution)/shard_map/ppermute | solution.py:362
  30.2 23.3 %collective-permute-start.23 = (bf16[2,256,128]{2,1,0:T(8,128)(2,1)S(1)}, bf16[2,256,128]{2,1,0:T(8,128)(2,1)S(1)}, u32[]{:S(2)}, u32[]{:S(2)}) collective-permute-start(bf16[2,256,128]{2,1,0:T(8,128)(2,1)S(1)} %shard_map.60.refs_17_), channel_id=1, source_target_pairs={{16,12},{17,13},{18,8},{19,9},{20,14},{21,15},{22,10},{23,11}} | collective-permute-start | bytes 393224 | tf_op jit(solution)/shard_map/ppermute | solution.py:362
  31.5 23.3 %collective-permute-start.22 = (bf16[2,256,128]{2,1,0:T(8,128)(2,1)S(1)}, bf16[2,256,128]{2,1,0:T(8,128)(2,1)S(1)}, u32[]{:S(2)}, u32[]{:S(2)}) collective-permute-start(bf16[2,256,128]{2,1,0:T(8,128)(2,1)S(1)} %shard_map.60.refs_17_), channel_id=1, source_target_pairs={{16,11},{17,10},{18,15},{19,14},{20,9},{21,8},{22,13},{23,12}} | collective-permute-start | bytes 393224 | tf_op jit(solution)/shard_map/ppermute | solution.py:362
  32.9 51.2 %collective-permute-start.17 = (bf16[4,2,256,128]{3,2,1,0:T(8,128)(2,1)S(1)}, bf16[4,2,256,128]{3,2,1,0:T(8,128)(2,1)S(1)}, u32[]{:S(2)}, u32[]{:S(2)}) collective-permute-start(bf16[4,2,256,128]{3,2,1,0:T(8,128)(2,1)S(1)} %pad_maximum_fusion.refs_0_), channel_id=1, source_target_pairs={{0,1},{1,0},{2,3},{3,2},{4,5},{5,4},{6,7},{7,6},{8,9},{9,8},{10,11... | collective-permute-start | bytes 1572872 | tf_op jit(solution)/shard_map/ppermute | solution.py:368
  48.1 8.1 %collective-permute-start.21 = (bf16[2,256,128]{2,1,0:T(8,128)(2,1)S(1)}, bf16[2,256,128]{2,1,0:T(8,128)(2,1)S(1)}, u32[]{:S(2)}, u32[]{:S(2)}) collective-permute-start(bf16[2,256,128]{2,1,0:T(8,128)(2,1)S(1)} %shard_map.60.refs_17_), channel_id=1, source_target_pairs={{16,10},{17,11},{18,14},{19,15},{20,8},{21,9},{22,12},{23,13}} | collective-permute-start | bytes 393224 | tf_op jit(solution)/shard_map/ppermute | solution.py:362
  51.2 10.0 %collective-permute-start.20 = (bf16[2,256,128]{2,1,0:T(8,128)(2,1)S(1)}, bf16[2,256,128]{2,1,0:T(8,128)(2,1)S(1)}, u32[]{:S(2)}, u32[]{:S(2)}) collective-permute-start(bf16[2,256,128]{2,1,0:T(8,128)(2,1)S(1)} %shard_map.60.refs_17_), channel_id=1, source_target_pairs={{16,15},{17,14},{18,13},{19,12},{20,11},{21,10},{22,9},{23,8}} | collective-permute-start | bytes 393224 | tf_op jit(solution)/shard_map/ppermute | solution.py:362
  53.5 9.5 %collective-permute-start.19 = (bf16[2,256,128]{2,1,0:T(8,128)(2,1)S(1)}, bf16[2,256,128]{2,1,0:T(8,128)(2,1)S(1)}, u32[]{:S(2)}, u32[]{:S(2)}) collective-permute-start(bf16[2,256,128]{2,1,0:T(8,128)(2,1)S(1)} %shard_map.60.refs_17_), channel_id=1, source_target_pairs={{16,9},{17,8},{18,11},{19,10},{20,13},{21,12},{22,15},{23,14}} | collective-permute-start | bytes 393224 | tf_op jit(solution)/shard_map/ppermute | solution.py:362
  54.8 9.1 %collective-permute-start.18 = (bf16[2,256,128]{2,1,0:T(8,128)(2,1)S(1)}, bf16[2,256,128]{2,1,0:T(8,128)(2,1)S(1)}, u32[]{:S(2)}, u32[]{:S(2)}) collective-permute-start(bf16[2,256,128]{2,1,0:T(8,128)(2,1)S(1)} %shard_map.60.refs_17_), channel_id=1, source_target_pairs={{16,14},{17,15},{18,12},{19,13},{20,10},{21,11},{22,8},{23,9}} | collective-permute-start | bytes 393224 | tf_op jit(solution)/shard_map/ppermute | solution.py:362
  65.9 8.1 %collective-permute-start.32 = (bf16[2,256,128]{2,1,0:T(8,128)(2,1)S(1)}, bf16[2,256,128]{2,1,0:T(8,128)(2,1)S(1)}, u32[]{:S(2)}, u32[]{:S(2)}) collective-permute-start(bf16[2,256,128]{2,1,0:T(8,128)(2,1)S(1)} %shard_map.62.refs_16_), channel_id=1, source_target_pairs={{8,7},{9,6},{10,5},{11,4},{12,3},{13,2},{14,1},{15,0}} | collective-permute-start | bytes 393224 | tf_op jit(solution)/shard_map/ppermute | solution.py:362
  67.2 11.6 %collective-permute-start.31 = (bf16[2,256,128]{2,1,0:T(8,128)(2,1)S(1)}, bf16[2,256,128]{2,1,0:T(8,128)(2,1)S(1)}, u32[]{:S(2)}, u32[]{:S(2)}) collective-permute-start(bf16[2,256,128]{2,1,0:T(8,128)(2,1)S(1)} %shard_map.62.refs_16_), channel_id=1, source_target_pairs={{8,1},{9,0},{10,3},{11,2},{12,5},{13,4},{14,7},{15,6}} | collective-permute-start | bytes 393224 | tf_op jit(solution)/shard_map/ppermute | solution.py:362
  68.5 11.6 %collective-permute-start.30 = (bf16[2,256,128]{2,1,0:T(8,128)(2,1)S(1)}, bf16[2,256,128]{2,1,0:T(8,128)(2,1)S(1)}, u32[]{:S(2)}, u32[]{:S(2)}) collective-permute-start(bf16[2,256,128]{2,1,0:T(8,128)(2,1)S(1)} %shard_map.62.refs_16_), channel_id=1, source_target_pairs={{8,6},{9,7},{10,4},{11,5},{12,2},{13,3},{14,0},{15,1}} | collective-permute-start | bytes 393224 | tf_op jit(solution)/shard_map/ppermute | solution.py:362
  69.8 17.4 %collective-permute-start.29 = (bf16[2,256,128]{2,1,0:T(8,128)(2,1)S(1)}, bf16[2,256,128]{2,1,0:T(8,128)(2,1)S(1)}, u32[]{:S(2)}, u32[]{:S(2)}) collective-permute-start(bf16[2,256,128]{2,1,0:T(8,128)(2,1)S(1)} %shard_map.62.refs_16_), channel_id=1, source_target_pairs={{8,0},{9,1},{10,2},{11,3},{12,4},{13,5},{14,6},{15,7}} | collective-permute-start | bytes 393224 | tf_op jit(solution)/shard_map/ppermute | solution.py:362
  74.1 13.2 %collective-permute-start.28 = (bf16[2,256,128]{2,1,0:T(8,128)(2,1)S(1)}, bf16[2,256,128]{2,1,0:T(8,128)(2,1)S(1)}, u32[]{:S(2)}, u32[]{:S(2)}) collective-permute-start(bf16[2,256,128]{2,1,0:T(8,128)(2,1)S(1)} %shard_map.62.refs_16_), channel_id=1, source_target_pairs={{8,5},{9,4},{10,1},{11,0},{12,7},{13,6},{14,3},{15,2}} | collective-permute-start | bytes 393224 | tf_op jit(solution)/shard_map/ppermute | solution.py:362
  78.8 8.5 %collective-permute-start.27 = (bf16[2,256,128]{2,1,0:T(8,128)(2,1)S(1)}, bf16[2,256,128]{2,1,0:T(8,128)(2,1)S(1)}, u32[]{:S(2)}, u32[]{:S(2)}) collective-permute-start(bf16[2,256,128]{2,1,0:T(8,128)(2,1)S(1)} %shard_map.62.refs_16_), channel_id=1, source_target_pairs={{8,4},{9,5},{10,0},{11,1},{12,6},{13,7},{14,2},{15,3}} | collective-permute-start | bytes 393224 | tf_op jit(solution)/shard_map/ppermute | solution.py:362
  (11 other events, 47.8 us)
